TPU v7x, 128 devices: a whole 4x4x4 slice. The times are simulated.
128 devices in a mesh: rep: 1, r: 16 (over y, z), s: 8 (over x, core).
Axes of the slice: x: 4, y: 4, z: 4, core: 2. Of those that a mesh axis runs over, the one named last changes fastest.
Arguments:
- x: bfloat16 [128, 2048, 640], P(('rep', 'r', 's'))
- dy: bfloat16 [128, 2048, 640], P(('rep', 'r', 's'))
- w_gate: bfloat16 [2, 640, 4096], P(None, 's')
- w_up: bfloat16 [2, 640, 4096], P(None, 's')
- w_down: bfloat16 [2, 4096, 640], P(None, 's')
Outputs:
- output 1: bfloat16 [128, 2048, 640], P(('rep', 'r', 's'))
- output 2: bfloat16 [2, 640, 4096], P('rep', 's')
- output 3: bfloat16 [2, 640, 4096], P('rep', 's')
- output 4: bfloat16 [2, 4096, 640], P('rep', 's')
All inputs are finite; a program needn't handle non-finite values.
Results may differ from a plain program's by a relative error of at most 0.018.
Values are sent between devices in bfloat16 or wider.
A program may use at most 1.5 GiB of HBM per device.

v0:
```python
import jax
import jax.numpy as jnp
from jax import lax
from jax.sharding import PartitionSpec as P

NAMES = ("w_gate", "w_up", "w_down")


def matmul(a, w):
    return jnp.dot(a, w, preferred_element_type=jnp.float32).astype(jnp.bfloat16)


def normed(h):
    wide = h.astype(jnp.float32)
    scale = lax.rsqrt(jnp.mean(wide**2, -1, keepdims=True) + 1e-6)
    return (wide * scale).astype(jnp.bfloat16)


def layer(h, w):
    a = normed(h)
    gate = jnp.dot(a, w["w_gate"], preferred_element_type=jnp.float32)
    up = jnp.dot(a, w["w_up"], preferred_element_type=jnp.float32)
    return h + matmul((jax.nn.silu(gate) * up).astype(jnp.bfloat16), w["w_down"])


def solution(mesh):
    def fetched(weights, number):
        return {name: lax.all_gather(w[number], "s", axis=0, tiled=True) for name, w in zip(NAMES, weights, strict=True)}

    def summed(term):
        return lax.psum(lax.psum_scatter(term, "s", scatter_dimension=0, tiled=True), "r")

    def step(x, dy, *weights):
        layers = weights[0].shape[0]
        h, inputs = x[0], []
        for number in range(layers):
            inputs.append(h)
            h = layer(h, fetched(weights, number))
        by_h, mine = dy[0], [None] * layers
        for number in reversed(range(layers)):
            _, back = jax.vjp(lambda w, h: layer(h, w), fetched(weights, number), inputs[number])
            by_w, by_h = back(by_h)
            mine[number] = [summed(by_w[name]) for name in NAMES]
        return (by_h[None], *(jnp.stack([mine[number][i] for number in range(layers)]) for i in range(3)))

    states, cut = P(("rep", "r", "s"), None, None), P(None, "s", None)
    return jax.shard_map(
        step,
        mesh=mesh,
        in_specs=(states, states) + (cut,) * 3,
        out_specs=(states,) + (P("rep", "s", None),) * 3,
        check_vma=False,
    )
```

profile of v0, /device:TPU:0, one launch (start us, length us, event | category | flops | bytes accessed | tf_op | source)
XLA Modules:
  0.0 718.8 jit_solution(10578060982974513772)
XLA Ops:
  7.2 0.0 all-gather.13.cloned.1.call-start
  7.2 2.5 fusion.86
  9.8 0.0 all-gather.13.cloned.1.call-update
  9.8 0.0 all-gather.15.cloned.1.call-start
  9.8 2.5 fusion.88
  12.3 0.0 all-gather.15.cloned.1.call-update
  12.3 0.0 all-gather.17.cloned.1.call-start
  12.4 1.2 fusion.87
  13.6 0.0 all-gather.17.cloned.1.call-update
  13.6 0.0 all-gather.21.cloned.1.call-start
  13.6 0.5 all-gather.21.cloned.1.call-update
  14.2 0.0 all-gather.23.cloned.1.call-start
  14.2 0.5 all-gather.23.cloned.1.call-update
  14.7 0.0 all-gather.19.cloned.1.call-start
  14.8 0.5 all-gather.19.cloned.1.call-update
  15.3 0.0 reduce-scatter.15.cloned.1.call-start
  15.4 3.0 copy.10
  18.4 0.6 fusion.18
  18.9 0.9 copy-done.8
  19.8 4.5 copy.9
  24.3 24.5 %all-gather.13.cloned.1.call-done = bf16[1,640,4096]{2,1,0:T(8,128)(2,1)} async-done(((bf16[1,80,4096]{2,1,0:T(8,128)(2,1)}), bf16[1,640,4096]{2,1,0:T(8,128)(2,1)}) %all-gather.13.cloned.1.call-update) | async-done | bytes 5242896 | tf_op jit(solution)/shard_map/all_gather | solution.py:28
  48.9 19.7 %fusion.40 = f32[2048,4096]{1,0:T(8,128)} fusion(bf16[1,640,4096]{2,1,0:T(8,128)(2,1)} %all-gather.13.cloned.1.call-done, bf16[1,2048,640]{1,2,0:T(8,128)(2,1)S(1)} %copy.10, f32[2048]{0:T(1024)S(1)} %fusion.79), kind=kOutput, calls=%fused_computation.65 | convolution fusion | flops 10741350400 | bytes 41426944 | tf_op jit(solution)/shard_map/dot_general | solution.py:21
  68.6 18.8 %all-gather.15.cloned.1.call-done = bf16[1,640,4096]{2,1,0:T(8,128)(2,1)} async-done(((bf16[1,80,4096]{2,1,0:T(8,128)(2,1)}), bf16[1,640,4096]{2,1,0:T(8,128)(2,1)}) %all-gather.15.cloned.1.call-update) | async-done | bytes 5242896 | tf_op jit(solution)/shard_map/all_gather | solution.py:28
  87.4 33.3 %multiply_convert_fusion.1 = (bf16[2048,4096]{1,0:T(8,128)(2,1)}, f32[2048,4096]{1,0:T(8,128)}) fusion(f32[2048,4096]{1,0:T(8,128)} %fusion.40, bf16[1,640,4096]{2,1,0:T(8,128)(2,1)} %all-gather.15.cloned.1.call-done, bf16[1,2048,640]{1,2,0:T(8,128)(2,1)S(1)} %copy.10, f32[2048]{0:T(1024)S(1)} %fusion.79), kind=kOutput, calls=%fused_computation.13 | convolution fusion | flops 10791682048 | bytes 91758592 | tf_op jit(solution)/shard_map/dot_general | solution.py:22
  120.7 4.6 all-gather.17.cloned.1.call-done
  125.4 17.9 %fusion.21 = (f32[2048]{0:T(1024)S(1)}, bf16[2048,640]{0,1:T(8,128)(2,1)}) fusion(bf16[2048,4096]{1,0:T(8,128)(2,1)} %get-tuple-element.20, bf16[1,4096,640]{2,1,0:T(8,128)(2,1)} %all-gather.17.cloned.1.call-done, bf16[1,2048,640]{1,2,0:T(8,128)(2,1)S(1)} %copy.10), kind=kOutput, calls=%fused_computation.46 | convolution fusion | flops 10743969792 | bytes 27271168 | tf_op jit(solution)/shard_map/dot_general | solution.py:10
  143.4 19.8 %all-gather.21.cloned.1.call-done = bf16[1,4096,640]{2,1,0:T(8,128)(2,1)} async-done(((bf16[1,512,640]{2,1,0:T(8,128)(2,1)}), bf16[1,4096,640]{2,1,0:T(8,128)(2,1)}) %all-gather.21.cloned.1.call-update) | async-done | bytes 5242896 | tf_op jit(solution)/shard_map/all_gather | solution.py:28
  163.2 19.6 %convolution_convert_fusion.1 = bf16[2048,4096]{1,0:T(8,128)(2,1)} fusion(bf16[1,4096,640]{2,1,0:T(8,128)(2,1)} %all-gather.21.cloned.1.call-done, bf16[1,2048,640]{2,1,0:T(8,128)(2,1)} %param.6), kind=kOutput, calls=%fused_computation.22 | convolution fusion | flops 10745806848 | bytes 24641536 | tf_op jit(solution)/shard_map/transpose(jvp())/dot_general | solution.py:10
  182.8 18.8 %all-gather.23.cloned.1.call-done = bf16[1,640,4096]{2,1,0:T(8,128)(2,1)} async-done(((bf16[1,80,4096]{2,1,0:T(8,128)(2,1)}), bf16[1,640,4096]{2,1,0:T(8,128)(2,1)}) %all-gather.23.cloned.1.call-update) | async-done | bytes 5242896 | tf_op jit(solution)/shard_map/all_gather | solution.py:28
  201.6 19.9 %fusion.24 = f32[2048,4096]{1,0:T(8,128)} fusion(bf16[1,640,4096]{2,1,0:T(8,128)(2,1)} %all-gather.23.cloned.1.call-done, bf16[2048,640]{0,1:T(8,128)(2,1)S(1)} %copy-done.5, f32[2048]{0:T(1024)S(1)} %fusion.80), kind=kOutput, calls=%fused_computation.49 | convolution fusion | flops 10741350400 | bytes 41426944 | tf_op jit(solution)/shard_map/jvp()/dot_general | solution.py:22
  221.5 18.5 %all-gather.19.cloned.1.call-done = bf16[1,640,4096]{2,1,0:T(8,128)(2,1)} async-done(((bf16[1,80,4096]{2,1,0:T(8,128)(2,1)}), bf16[1,640,4096]{2,1,0:T(8,128)(2,1)}) %all-gather.19.cloned.1.call-update) | async-done | bytes 5242896 | tf_op jit(solution)/shard_map/all_gather | solution.py:28
  240.0 42.6 %fusion.1 = (bf16[2048,4096]{1,0:T(8,128)(2,1)}, f32[2048,4096]{1,0:T(8,128)}) fusion(f32[2048,4096]{1,0:T(8,128)} %fusion.24, bf16[2048,4096]{1,0:T(8,128)(2,1)} %convolution_convert_fusion.1, bf16[1,640,4096]{2,1,0:T(8,128)(2,1)} %all-gather.19.cloned.1.call-done, bf16[2048,640]{0,1:T(8,128)(2,1)S(1)} %copy-done.5, f32[2048]{0:T(1024)S(1)} %fusion.80), kind=kOutput, calls=%fused_computation.7 | convolution fusion | flops 10842013696 | bytes 108535808 | tf_op jit(solution)/shard_map/jvp()/dot_general | solution.py:21
  282.5 21.1 %fusion.51 = bf16[2048,640]{0,1:T(8,128)(2,1)S(1)} fusion(bf16[1,640,4096]{2,1,0:T(8,128)(2,1)} %all-gather.23.cloned.1.call-done, bf16[2048,4096]{1,0:T(8,128)(2,1)} %convolution_convert_fusion.1, f32[2048,4096]{1,0:T(8,128)} %get-tuple-element.25), kind=kOutput, calls=%fused_computation.70 | convolution fusion | flops 10789060608 | bytes 58195968 | tf_op jit(solution)/shard_map/transpose(jvp())/dot_general | solution.py:22
  303.7 15.1 %fusion.23 = (f32[2048]{0:T(1024)S(1)}, bf16[2048,640]{0,1:T(8,128)(2,1)S(1)}) fusion(bf16[2048,640]{0,1:T(8,128)(2,1)S(1)} %copy-done.5, bf16[2048,640]{0,1:T(8,128)(2,1)S(1)} %fusion.51, bf16[2048,4096]{1,0:T(8,128)(2,1)} %get-tuple-element.24, bf16[1,640,4096]{2,1,0:T(8,128)(2,1)S(1)} %copy-done.16), kind=kOutput, calls=%fused_computation.48 | convolution fusion | flops 10743969792 | bytes 29892608 | tf_op jit(solution)/shard_map/transpose(jvp())/dot_general | solution.py:21
  318.8 1.8 fusion.68
  320.7 1.5 copy-done.2
  322.1 19.3 %convolution_convert_fusion.2 = bf16[4096,640]{1,0:T(8,128)(2,1)} fusion(bf16[2048,4096]{1,0:T(8,128)(2,1)} %get-tuple-element.20, bf16[2048,640]{0,1:T(8,128)(2,1)S(1)} %fusion.68), kind=kOutput, calls=%fused_computation.33 | convolution fusion | flops 10740039680 | bytes 24641536 | tf_op jit(solution)/shard_map/transpose(jvp())/dot_general | solution.py:10
  341.5 0.0 reduce-scatter.17.cloned.1.call-start
  341.5 1.7 copy-done.6
  343.2 27.6 %fusion.11 = bf16[4096,640]{1,0:T(8,128)(2,1)} fusion(f32[2048,4096]{1,0:T(8,128)} %fusion.24, bf16[1,2048,640]{2,1,0:T(8,128)(2,1)S(1)} %copy-done.6, f32[2048,4096]{1,0:T(8,128)} %get-tuple-element.25), kind=kOutput, calls=%fused_computation.34 | convolution fusion | flops 10790371328 | bytes 74973184 | tf_op jit(solution)/shard_map/transpose(jvp())/dot_general | solution.py:10
  370.8 0.0 reduce-scatter.11.cloned.1.call-start
  370.9 41.6 %fusion.3 = (bf16[2048,4096]{1,0:T(8,128)(2,1)}, bf16[2048,4096]{1,0:T(8,128)(2,1)}) fusion(f32[2048,4096]{1,0:T(8,128)} %fusion.40, f32[2048,4096]{1,0:T(8,128)} %get-tuple-element.21, bf16[2048,640]{0,1:T(8,128)(2,1)} %copy-done.2, bf16[1,4096,640]{2,1,0:T(8,128)(2,1)} %all-gather.17.cloned.1.call-done), kind=kOutput, calls=%fused_computation.9 | convolution fusion | flops 10846470144 | bytes 108527616 | tf_op jit(solution)/shard_map/transpose(jvp())/dot_general | solution.py:10
  412.5 23.0 %fusion.12 = bf16[640,4096]{1,0:T(8,128)(2,1)} fusion(bf16[2048,4096]{1,0:T(8,128)(2,1)} %get-tuple-element.29, bf16[1,2048,640]{1,2,0:T(8,128)(2,1)S(1)} %copy-done.1, f32[2048]{0:T(1024)S(1)} %copy-done.11, f32[2048,4096]{1,0:T(8,128)} %fusion.40), kind=kOutput, calls=%fused_computation.35 | convolution fusion | flops 10794303488 | bytes 58204160 | tf_op jit(solution)/shard_map/transpose(jvp())/dot_general | solution.py:22
  435.5 0.0 reduce-scatter.13.cloned.1.call-start
  435.5 0.6 copy-done.13
  436.1 24.0 %fusion.13 = bf16[640,4096]{1,0:T(8,128)(2,1)} fusion(bf16[2048,4096]{1,0:T(8,128)(2,1)} %convolution_convert_fusion.1, bf16[2048,640]{0,1:T(8,128)(2,1)} %get-tuple-element.23, f32[2048]{0:T(1024)S(1)} %copy-done.13, f32[2048,4096]{1,0:T(8,128)} %get-tuple-element.25), kind=kOutput, calls=%fused_computation.36 | convolution fusion | flops 10794303488 | bytes 58204160 | tf_op jit(solution)/shard_map/transpose(jvp())/dot_general | solution.py:22
  460.1 0.0 reduce-scatter.9.cloned.1.call-start
  460.2 16.8 %convolution_convert_fusion.3 = bf16[640,4096]{1,0:T(8,128)(2,1)} fusion(bf16[2048,4096]{1,0:T(8,128)(2,1)} %get-tuple-element.24, bf16[2048,640]{0,1:T(8,128)(2,1)} %get-tuple-element.23, f32[2048]{0:T(1024)S(1)} %copy-done.13), kind=kOutput, calls=%fused_computation.37 | convolution fusion | flops 10741350400 | bytes 24649728 | tf_op jit(solution)/shard_map/transpose(jvp())/dot_general | solution.py:21
  477.0 0.0 reduce-scatter.7.cloned.1.call-start
  477.1 16.1 %convolution_convert_fusion.4 = bf16[640,4096]{1,0:T(8,128)(2,1)} fusion(bf16[2048,4096]{1,0:T(8,128)(2,1)} %get-tuple-element.28, bf16[1,2048,640]{1,2,0:T(8,128)(2,1)S(1)} %copy-done.1, f32[2048]{0:T(1024)S(1)} %copy-done.11), kind=kOutput, calls=%fused_computation.38 | convolution fusion | flops 10741350400 | bytes 24649728 | tf_op jit(solution)/shard_map/transpose(jvp())/dot_general | solution.py:21
  493.1 0.0 all-reduce.3.cloned.1.call-start
  493.2 0.0 reduce-scatter.15.cloned.1.call-done
  493.2 0.0 reduce-scatter.17.cloned.1.call-done
  493.2 0.0 reduce-scatter.11.cloned.1.call-done
  493.3 24.1 %reduce-scatter.13.cloned.1.call-done = bf16[80,4096]{1,0:T(8,128)(2,1)} async-done(((bf16[640,4096]{1,0:T(8,128)(2,1)}), bf16[80,4096]{1,0:T(8,128)(2,1)}) %reduce-scatter.13.cloned.1.call-update) | async-done | bytes 655376 | tf_op jit(solution)/shard_map/reduce_scatter | solution.py:31
  517.4 41.8 %reduce-scatter.9.cloned.1.call-done = bf16[80,4096]{1,0:T(8,128)(2,1)} async-done(((bf16[640,4096]{1,0:T(8,128)(2,1)}), bf16[80,4096]{1,0:T(8,128)(2,1)}) %reduce-scatter.9.cloned.1.call-update) | async-done | bytes 655376 | tf_op jit(solution)/shard_map/reduce_scatter | solution.py:31
  559.2 41.7 %reduce-scatter.7.cloned.1.call-done = bf16[80,4096]{1,0:T(8,128)(2,1)} async-done(((bf16[640,4096]{1,0:T(8,128)(2,1)}), bf16[80,4096]{1,0:T(8,128)(2,1)}) %reduce-scatter.7.cloned.1.call-update) | async-done | bytes 655376 | tf_op jit(solution)/shard_map/reduce_scatter | solution.py:31
  600.9 20.9 %fusion.48 = bf16[2048,640]{0,1:T(8,128)(2,1)S(1)} fusion(bf16[1,640,4096]{2,1,0:T(8,128)(2,1)} %all-gather.15.cloned.1.call-done, bf16[2048,4096]{1,0:T(8,128)(2,1)} %get-tuple-element.29, f32[2048,4096]{1,0:T(8,128)} %fusion.40), kind=kOutput, calls=%fused_computation.69 | convolution fusion | flops 10789060608 | bytes 58195968 | tf_op jit(solution)/shard_map/transpose(jvp())/dot_general | solution.py:22
  621.8 16.5 %fusion.20 = (f32[2048]{0:T(1024)S(1)}, bf16[2048,640]{0,1:T(8,128)(2,1)S(1)}) fusion(bf16[1,2048,640]{1,2,0:T(8,128)(2,1)S(1)} %copy-done.1, bf16[2048,640]{0,1:T(8,128)(2,1)S(1)} %fusion.48, bf16[2048,4096]{1,0:T(8,128)(2,1)} %get-tuple-element.28, bf16[1,640,4096]{2,1,0:T(8,128)(2,1)} %all-gather.13.cloned.1.call-done), kind=kOutput, calls=%fused_computation.45 | convolution fusion | flops 10743969792 | bytes 29892608 | tf_op jit(solution)/shard_map/transpose(jvp())/dot_general | solution.py:21
  638.4 3.3 fusion.67
  641.7 4.4 copy.11
  646.0 59.9 %all-reduce.3.cloned.1.call-done = (bf16[1,80,4096]{2,1,0:T(8,128)(2,1)}, bf16[1,80,4096]{2,1,0:T(8,128)(2,1)}, bf16[1,80,4096]{2,1,0:T(8,128)(2,1)}, bf16[1,80,...) async-done(((bf16[1,80,4096]{2,1,0:T(8,128)(2,1)}, bf16[1,80,4096]{2,1,0:T(8,128)(2,1)}, bf16[1,80,4096]{2,1,0:T(8,128)(2,1)}, ...) | async-done | bytes 3932176 | tf_op jit(solution)/shard_map/psum | solution.py:31
  705.9 2.5 pad_maximum_fusion.2
  708.4 3.4 pad_maximum_fusion
  (41 shorter events, 0.2 us)
Async XLA Ops:
  7.2 5.2 copy-start.7
  7.2 41.7 %all-gather.13.cloned.1.call-start = ((), (), s32[]{:S(2)}) async-start(), calls=%async_computation.12 | async-start | bytes 5898240 | tf_op jit(solution)/shard_map/all_gather | solution.py:28
  9.8 77.6 %all-gather.15.cloned.1.call-start = ((), (), s32[]{:S(2)}) async-start(), calls=%async_computation.13 | async-start | bytes 5898240 | tf_op jit(solution)/shard_map/all_gather | solution.py:28
  12.3 113.1 %all-gather.17.cloned.1.call-start = ((), (), s32[]{:S(2)}) async-start(), calls=%async_computation.14 | async-start | bytes 5898240 | tf_op jit(solution)/shard_map/all_gather | solution.py:28
  13.6 149.6 %all-gather.21.cloned.1.call-start = ((), (), s32[]{:S(2)}) async-start(), calls=%async_computation.16 | async-start | bytes 5898240 | tf_op jit(solution)/shard_map/all_gather | solution.py:28
  14.2 187.4 %all-gather.23.cloned.1.call-start = ((), (), s32[]{:S(2)}) async-start(), calls=%async_computation.17 | async-start | bytes 5898240 | tf_op jit(solution)/shard_map/all_gather | solution.py:28
  14.7 225.2 %all-gather.19.cloned.1.call-start = ((), (), s32[]{:S(2)}) async-start(), calls=%async_computation.15 | async-start | bytes 5898240 | tf_op jit(solution)/shard_map/all_gather | solution.py:28
  15.3 477.9 %reduce-scatter.15.cloned.1.call-start = ((), (), s32[]{:S(2)}) async-start(), calls=%async_computation.10 | async-start | bytes 5898240 | tf_op jit(solution)/shard_map/reduce_scatter | solution.py:31
  18.4 107.0 %copy-start = (bf16[1,2048,640]{1,2,0:T(8,128)(2,1)}, bf16[1,2048,640]{1,2,0:T(8,128)(2,1)S(1)}, u32[]{:S(2)}) copy-start(bf16[1,2048,640]{1,2,0:T(8,128)(2,1)S(1)} %copy.10) | copy-start | bytes 7864324
  18.9 0.9 copy-start.8
  19.8 67.6 %copy-start.10 = (f32[2048]{0:T(1024)}, f32[2048]{0:T(1024)S(1)}, u32[]{:S(2)}) copy-start(f32[2048]{0:T(1024)S(1)} %fusion.79) | copy-start | bytes 24580
  143.3 39.4 %copy-start.14 = (f32[2048]{0:T(1024)}, f32[2048]{0:T(1024)S(1)}, u32[]{:S(2)}) copy-start(f32[2048]{0:T(1024)S(1)} %get-tuple-element.22) | copy-start | bytes 24580
  143.3 175.5 %copy-start.12 = (f32[2048]{0:T(1024)}, f32[2048]{0:T(1024)S(1)}, u32[]{:S(2)}) copy-start(f32[2048]{0:T(1024)S(1)} %fusion.80) | copy-start | bytes 24580
  143.3 58.2 %copy-start.5 = (bf16[2048,640]{0,1:T(8,128)(2,1)S(1)}, bf16[2048,640]{0,1:T(8,128)(2,1)}, u32[]{:S(2)}) copy-start(bf16[2048,640]{0,1:T(8,128)(2,1)} %get-tuple-element.23) | copy-start | bytes 7864324
  282.5 21.1 %copy-start.16 = (bf16[1,640,4096]{2,1,0:T(8,128)(2,1)S(1)}, bf16[1,640,4096]{2,1,0:T(8,128)(2,1)}, u32[]{:S(2)}) copy-start(bf16[1,640,4096]{2,1,0:T(8,128)(2,1)} %all-gather.19.cloned.1.call-done) | copy-start | bytes 15728644
  303.7 15.1 %copy-start.15 = (f32[2048]{0:T(1024)S(1)}, f32[2048]{0:T(1024)}, u32[]{:S(2)}) copy-start(f32[2048]{0:T(1024)} %copy-done.14) | copy-start | bytes 24580
  303.7 15.1 %copy-start.4 = (bf16[1,2048,640]{1,2,0:T(8,128)(2,1)S(1)}, bf16[1,2048,640]{1,2,0:T(8,128)(2,1)}, u32[]{:S(2)}) copy-start(bf16[1,2048,640]{1,2,0:T(8,128)(2,1)} %copy.9) | copy-start | bytes 7864324
  320.7 1.5 copy-start.2
  341.4 1.7 copy-start.6
  341.5 151.8 %reduce-scatter.17.cloned.1.call-start = ((), (), s32[]{:S(2)}) async-start(), calls=%async_computation.11 | async-start | bytes 5898240 | tf_op jit(solution)/shard_map/reduce_scatter | solution.py:31
  370.8 122.5 %reduce-scatter.11.cloned.1.call-start = ((), (), s32[]{:S(2)}) async-start(), calls=%async_computation.8 | async-start | bytes 5898240 | tf_op jit(solution)/shard_map/reduce_scatter | solution.py:31
  370.9 41.6 %copy-start.1 = (bf16[1,2048,640]{1,2,0:T(8,128)(2,1)S(1)}, bf16[1,2048,640]{1,2,0:T(8,128)(2,1)}, u32[]{:S(2)}) copy-start(bf16[1,2048,640]{1,2,0:T(8,128)(2,1)} %copy-done) | copy-start | bytes 7864324
  370.9 41.6 %copy-start.11 = (f32[2048]{0:T(1024)S(1)}, f32[2048]{0:T(1024)}, u32[]{:S(2)}) copy-start(f32[2048]{0:T(1024)} %copy-done.10) | copy-start | bytes 24580
  435.4 0.7 copy-start.13
  435.5 81.9 %reduce-scatter.13.cloned.1.call-start = ((), (), s32[]{:S(2)}) async-start(), calls=%async_computation.9 | async-start | bytes 5898240 | tf_op jit(solution)/shard_map/reduce_scatter | solution.py:31
  460.1 99.1 %reduce-scatter.9.cloned.1.call-start = ((), (), s32[]{:S(2)}) async-start(), calls=%async_computation.7 | async-start | bytes 5898240 | tf_op jit(solution)/shard_map/reduce_scatter | solution.py:31
  477.0 123.9 %reduce-scatter.7.cloned.1.call-start = ((), (), s32[]{:S(2)}) async-start(), calls=%async_computation.6 | async-start | bytes 5898240 | tf_op jit(solution)/shard_map/reduce_scatter | solution.py:31
  493.1 212.8 %all-reduce.3.cloned.1.call-start = ((), (), s32[]{:S(2)}) async-start(), calls=%async_computation.18 | async-start | bytes 7864320 | tf_op jit(solution)/shard_map/psum | solution.py:31
  621.8 16.5 %copy-start.9 = (f32[2048]{0:T(1024)S(1)}, f32[2048]{0:T(1024)}, u32[]{:S(2)}) copy-start(f32[2048]{0:T(1024)} %copy-done.8) | copy-start | bytes 24580
  621.8 16.6 %copy-start.3 = (bf16[2048,640]{0,1:T(8,128)(2,1)S(1)}, bf16[2048,640]{0,1:T(8,128)(2,1)}, u32[]{:S(2)}) copy-start(bf16[2048,640]{0,1:T(8,128)(2,1)} %copy-done.2) | copy-start | bytes 7864324
Sparse Core Ops, SparseCore 0:
  10.2 38.5 all-gather.12
  51.1 36.2 all-gather.14
  89.1 36.2 all-gather.16
  126.9 36.2 all-gather.20
  165.3 36.2 all-gather.22
  203.7 36.2 all-gather.18
  341.6 40.0 reduce-scatter.14
  384.1 39.3 reduce-scatter.16
  435.6 40.0 reduce-scatter.10
  478.0 39.3 reduce-scatter.12
  519.8 39.3 reduce-scatter.8
  561.5 39.3 reduce-scatter.6
  605.1 100.7 all-reduce.2
where the time goes:
time: 727 us; the launch traced here: 719 us
  matrix products  395 us (54%)
  waiting for transfers between devices  274 us (38%)
  local copies, waits for them, and re-layouts  22.8 us (3%)
  between operations  14.6 us (2%)
  other arithmetic  11.6 us (2%)
    dot_general x6, matrix products, layer(): up = jnp.dot(a, w['w_up'], preferred_element_type=jnp.float32)  142 us
    dot_general x6, matrix products, layer(): gate = jnp.dot(a, w['w_gate'], preferred_element_type=jnp.float32)  127 us
    dot_general x5, matrix products, matmul(): jnp.dot(a, w, preferred_element_type=jnp.float32).astype(jnp.bfloat16)  126 us
    reduce_scatter x6, waiting for transfers between devices, summed(): lax.psum_scatter(term, 's', scatter_dimension=0, tiled=True)  108 us
    all_gather x6, waiting for transfers between devices, fetched(): lax.all_gather(w[number], 's', axis=0, tiled=True)  105 us
    psum x1, waiting for transfers between devices, summed(): lax.psum(lax.psum_scatter(term, 's', scatter_dimension=0, tiled=True), 'r')  59.9 us
    unnamed x37, local copies, waits for them, and re-layouts  16.6 us
  transfers between devices with their start and end apart: 13, of which 10 were waited for; matrix products, arithmetic and copies ran while one was open for 44% of the time, Pallas kernels for 0%

commit v1 on v0

v1 whole, which is shorter than its diff:
```python
import functools

import jax
import jax.numpy as jnp
from jax import lax
from jax.experimental import pallas as pl
from jax.experimental.pallas import tpu as pltpu
from jax.sharding import PartitionSpec as P

NAMES = ("w_gate", "w_up", "w_down")
F32, BF16 = jnp.float32, jnp.bfloat16


def matmul(a, w):
    return jnp.dot(a, w, preferred_element_type=jnp.float32).astype(jnp.bfloat16)


def normed(h):
    wide = h.astype(jnp.float32)
    scale = lax.rsqrt(jnp.mean(wide**2, -1, keepdims=True) + 1e-6)
    return (wide * scale).astype(jnp.bfloat16)


def layer(h, w):
    a = normed(h)
    gate = jnp.dot(a, w["w_gate"], preferred_element_type=jnp.float32)
    up = jnp.dot(a, w["w_up"], preferred_element_type=jnp.float32)
    return h + matmul((jax.nn.silu(gate) * up).astype(jnp.bfloat16), w["w_down"])


class Place:
    def __init__(self):
        s, r = lax.axis_index("s"), lax.axis_index("r")
        self.rep = lax.axis_index("rep")
        self.x, self.c, self.y, self.z = s // 2, s % 2, r // 4, r % 4
        self.at = {"x": self.x, "y": self.y, "z": self.z}

    def device(self, axis=None, by=0):
        at = dict(self.at)
        c = self.c
        if axis is None:
            c = 1 - c
        else:
            at[axis] = (at[axis] + by) % 4
        return (self.rep, at["y"] * 4 + at["z"], at["x"] * 2 + c)

    def barrier(self):
        semaphore = pltpu.get_barrier_semaphore()
        for who in [self.device()] + [self.device(a, by) for a in "xyz" for by in (1, 3)]:
            pl.semaphore_signal(semaphore, inc=1, device_id=who, device_id_type=pl.DeviceIdType.MESH)
        pl.semaphore_wait(semaphore, 7)


class Sender:
    def __init__(self, send, recv):
        self.send, self.recv, self.n, self.started = send, recv, 0, []

    def copy(self, src, dst, who):
        k, self.n = self.n, self.n + 1
        made = pltpu.make_async_remote_copy(
            src_ref=src,
            dst_ref=dst,
            send_sem=self.send.at[k],
            recv_sem=self.recv.at[k],
            device_id=who,
            device_id_type=pl.DeviceIdType.MESH,
        )
        made.start()
        self.started.append(made)
        return made

    def finish(self):
        for made in self.started:
            made.wait_send()


class Part:
    def __init__(self, own, out, axis, dim, base, size):
        self.own, self.out, self.axis, self.dim, self.base, self.size = own, out, axis, dim, base, size

    def cut(self, q, half):
        w = self.size // 4
        start = self.base + q * w
        if half is not None:
            w //= 2
            start = start + half * w
        if isinstance(start, int):
            return pl.ds(start, w)
        return pl.ds(pl.multiple_of(start, w), w)

    def mine(self, q, half=None):
        d = self.cut(q, half)
        return self.own.at[:, d] if self.dim else self.own.at[d]

    def there(self, x, c, q, half=None):
        d = self.cut(q, half)
        return self.out.at[x, c, :, d] if self.dim else self.out.at[x, c, d]


GATHER_COPIES = 3 + 4 * 32


def gather_kernel(g, u, d, og, ou, od, send, recv, local):
    me = Place()
    x, c = me.x, me.c
    here = []
    for i, (own, out) in enumerate(((g, og), (u, ou), (d, od))):
        here.append(pltpu.make_async_copy(own, out.at[x, c], local.at[i]))
        here[-1].start()
    me.barrier()
    go = Sender(send, recv)
    other = me.device()
    columns, rows = g.shape[1], d.shape[0]
    parts = [
        Part(g, og, "y", 1, 0, columns // 2),
        Part(g, og, "z", 1, columns // 2, columns // 2),
        Part(u, ou, "y", 1, 0, columns),
        Part(d, od, "z", 0, 0, rows),
    ]
    x1, x2, x3 = (x + 1) % 4, (x + 2) % 4, (x + 3) % 4
    across = []
    first = []
    for p in parts:
        q = me.at[p.axis]
        first.append(
            (
                go.copy(p.mine(q), p.there(x, c, q), me.device("x", 1)),
                go.copy(p.mine(q), p.there(x, c, q), me.device("x", 3)),
            )
        )
    for own, out in ((g, og), (u, ou), (d, od)):
        across.append(go.copy(own, out.at[x, c], other))
    second, along = [], []
    for p, (left, right) in zip(parts, first):
        q = me.at[p.axis]
        up, down = me.device(p.axis, 1), me.device(p.axis, 3)
        left.wait_recv()
        a = go.copy(p.there(x3, c, q, 0), p.there(x3, c, q, 0), me.device("x", 1))
        l = [go.copy(p.there(x3, c, q), p.there(x3, c, q), who) for who in (up, down)]
        across.append(go.copy(p.there(x3, c, q), p.there(x3, c, q), other))
        right.wait_recv()
        b = go.copy(p.there(x1, c, q, 1), p.there(x1, c, q, 1), me.device("x", 3))
        r = [go.copy(p.there(x1, c, q), p.there(x1, c, q), who) for who in (up, down)]
        across.append(go.copy(p.there(x1, c, q), p.there(x1, c, q), other))
        second.append((a, b))
        along.append([(x3, l), (x1, r)])
    for p, (a, b), l in zip(parts, second, along):
        q = me.at[p.axis]
        up, down = me.device(p.axis, 1), me.device(p.axis, 3)
        a.wait_recv()
        b.wait_recv()
        l.append((x2, [go.copy(p.there(x2, c, q), p.there(x2, c, q), who) for who in (up, down)]))
        across.append(go.copy(p.there(x2, c, q), p.there(x2, c, q), other))
    last = []
    for k in range(3):
        for p, l in zip(parts, along):
            q = me.at[p.axis]
            q1, q3 = (q + 1) % 4, (q + 3) % 4
            up, down = me.device(p.axis, 1), me.device(p.axis, 3)
            at, (below, above) = l[k]
            below.wait_recv()
            last.append((p, at, 0, go.copy(p.there(at, c, q3, 0), p.there(at, c, q3, 0), up)))
            across.append(go.copy(p.there(at, c, q3), p.there(at, c, q3), other))
            above.wait_recv()
            last.append((p, at, 1, go.copy(p.there(at, c, q1, 1), p.there(at, c, q1, 1), down)))
            across.append(go.copy(p.there(at, c, q1), p.there(at, c, q1), other))
    for p, at, half, made in last:
        q2 = (me.at[p.axis] + 2) % 4
        made.wait_recv()
        across.append(go.copy(p.there(at, c, q2, half), p.there(at, c, q2, half), other))
    for made in across:
        made.wait_recv()
    for made in here:
        made.wait()
    go.finish()


def gathered(g, u, d):
    vmem, hbm = pl.BlockSpec(memory_space=pltpu.VMEM), pl.BlockSpec(memory_space=pltpu.HBM)
    out = pl.pallas_call(
        gather_kernel,
        out_shape=[jax.ShapeDtypeStruct((4, 2, *w.shape), w.dtype) for w in (g, u, d)],
        in_specs=[vmem] * 3,
        out_specs=[hbm] * 3,
        scratch_shapes=[
            pltpu.SemaphoreType.DMA((GATHER_COPIES,)),
            pltpu.SemaphoreType.DMA((GATHER_COPIES,)),
            pltpu.SemaphoreType.DMA((3,)),
        ],
        compiler_params=pltpu.CompilerParams(collective_id=0, has_side_effects=True),
        name="gather_weights",
    )(g, u, d)
    return [o.reshape(8 * o.shape[2], o.shape[3]) for o in out]


def added(dst, *srcs):
    shape = dst.shape
    if len(shape) == 3:
        for i in range(shape[0]):
            added(dst.at[i], *(s.at[i] for s in srcs))
        return
    rows, columns = shape
    step = 16 if rows % 16 == 0 else rows
    wide = min(columns, 1024)

    @pl.loop(0, rows // step)
    def _(i):
        for j in range(0, columns, wide):
            at = (pl.ds(pl.multiple_of(i * step, step), step), pl.ds(j, min(wide, columns - j)))
            total = srcs[0][at].astype(F32)
            for s in srcs[1:]:
                total = total + s[at].astype(F32)
            dst[at] = total.astype(dst.dtype)


class Ring:
    def __init__(self, me, go, axis, terms, cut, out, got, hold):
        self.me, self.go, self.terms, self.cut, self.out, self.got, self.hold = me, go, terms, cut, out, got, hold
        self.p = me.at[axis]
        self.up, self.down = me.device(axis, 1), me.device(axis, 3)

    def term(self, k, half):
        return [self.cut(t, (self.p + k) % 4, half) for t in self.terms]

    def send(self, slot, k, half, who, *more):
        held = self.hold.at[slot]
        added(held, *self.term(k, half), *more)
        return self.go.copy(held, self.got.at[slot], who)

    def start(self):
        self.far = (self.send(0, 2, 0, self.up), self.send(1, 2, 1, self.down))
        self.near = [self.send(2, 1, 1, self.up), self.send(3, 3, 0, self.down)]

    def middle(self):
        self.far[0].wait_recv()
        self.near.append(self.send(4, 1, 0, self.up, self.got.at[0]))
        self.far[1].wait_recv()
        self.near.append(self.send(5, 3, 1, self.down, self.got.at[1]))

    def end(self, cut_out):
        for made in self.near:
            made.wait_recv()
        added(cut_out(self.out, 0), *self.term(0, 0), self.got.at[3], self.got.at[4])
        added(cut_out(self.out, 1), *self.term(0, 1), self.got.at[2], self.got.at[5])


def piece(dim, n):
    def cut(ref, q, half):
        w = ref.shape[dim] // 4
        at = [slice(None)] * len(ref.shape)
        if n == dim:
            at[dim] = pl.ds(pl.multiple_of(q * w + half * (w // 2), w // 2), w // 2)
        else:
            at[dim] = pl.ds(pl.multiple_of(q * w, w), w)
            h = ref.shape[n] // 2
            at[n] = pl.ds(half * h, h)
        if dim == 0 and len(ref.shape) == 3:
            at[0] = q
        return ref.at[tuple(at)]

    return cut


def halves(n):
    def cut(ref, half):
        h = ref.shape[n] // 2
        at = [slice(None)] * len(ref.shape)
        at[n] = pl.ds(half * h, h)
        return ref.at[tuple(at)]

    return cut


ROUTES = (
    (1, (("x", 0, 2), ("y", 1, 1), ("z", 1, 1))),
    (1, (("y", 2, 0), ("z", 2, 0), ("x", 0, 2))),
    (0, (("z", 1, 0), ("x", 0, 1), ("y", 0, 0))),
)


def plan(shape, steps):
    sizes = []
    for _, dim, n in steps:
        cut = list(shape)
        if dim == 0 and len(cut) == 3:
            cut = cut[1:]
            whole = list(cut)
            cut[n - 1] //= 2
        else:
            cut[dim] //= 4
            whole = list(cut)
            cut[n] //= 2
        sizes.append((tuple(cut), tuple(whole)))
        shape = tuple(whole)
    return sizes


REDUCE_COPIES = 3 * (1 + 18 + 3 + 4)


def reduce_kernel(*refs):
    terms, outs, scratch = refs[:3], refs[3:6], list(refs[6:])
    send, recv, local = scratch[-3:]
    per = (len(scratch) - 3) // 3
    me = Place()
    c = me.c
    here = []
    for m in range(3):
        own = scratch[m * per]
        here.append(pltpu.make_async_copy(terms[m].at[:, c], own, local.at[m]))
        here[-1].start()
    me.barrier()
    go = Sender(send, recv)
    other = me.device()
    swaps = [go.copy(terms[m].at[:, 1 - c], scratch[m * per + 1], other) for m in range(3)]
    rings = [None] * 3
    for m in range(3):
        b = scratch[m * per : (m + 1) * per]
        axis, dim, n = ROUTES[m][1][0]
        here[m].wait()
        swaps[m].wait_recv()
        rings[m] = Ring(me, go, axis, (b[0], b[1]), piece(dim, n), b[2], b[3], b[4])
        rings[m].start()
    for step in range(3):
        for m in range(3):
            rings[m].middle()
        for m in range(3):
            b = scratch[m * per : (m + 1) * per]
            axis, dim, n = ROUTES[m][1][step]
            drop = dim == 0 and len(rings[m].terms[0].shape) == 3
            rings[m].end(halves(n - 1 if drop else n))
            if step < 2:
                axis, dim, n = ROUTES[m][1][step + 1]
                nxt = b[2 + 3 * (step + 1) :]
                rings[m] = Ring(me, go, axis, (b[2 + 3 * step],), piece(dim, n), nxt[0], nxt[1], nxt[2])
                rings[m].start()
    state = []
    for m in range(3):
        dim = ROUTES[m][0]
        b = scratch[m * per : (m + 1) * per]
        total, done = b[8], b[11]
        high, low = ("z", "y") if m == 2 else ("y", "z")
        size = done.shape[dim] // 16

        def at(hi, lo=None, half=None, done=done, dim=dim, size=size):
            w = size if lo is not None else 4 * size
            start = hi * (4 * size) + (lo * size if lo is not None else 0)
            if half is not None:
                w //= 2
                start = start + half * w
            d = pl.ds(pl.multiple_of(start, w), w)
            return done.at[:, d] if dim else done.at[d]

        h, l = me.at[high], me.at[low]
        added(at(h, l), total)
        made = [go.copy(at(h, l), at(h, l), me.device(low, k)) for k in (1, 2, 3)]
        state.append((at, high, h, made))
    near = []
    for at, high, h, made in state:
        for k in made:
            k.wait_recv()
        near.append((go.copy(at(h), at(h), me.device(high, 1)), go.copy(at(h), at(h), me.device(high, 3))))
    last = []
    for (at, high, h, _), (below, above) in zip(state, near):
        h1, h3 = (h + 1) % 4, (h + 3) % 4
        below.wait_recv()
        last.append(go.copy(at(h3, None, 0), at(h3, None, 0), me.device(high, 1)))
        above.wait_recv()
        last.append(go.copy(at(h1, None, 1), at(h1, None, 1), me.device(high, 3)))
    for made in last:
        made.wait_recv()
    out = []
    for m in range(3):
        out.append(pltpu.make_async_copy(scratch[m * per + 11], outs[m], local.at[3 + m]))
        out[-1].start()
    for made in out:
        made.wait()
    go.finish()


def reduced(terms):
    terms = [t.reshape(4, 2, t.shape[0] // 8, t.shape[1]) for t in terms]
    scratch = []
    for m, t in enumerate(terms):
        block = (4, *t.shape[2:])
        scratch += [pltpu.VMEM(block, BF16)] * 2
        for half, whole in plan(block, ROUTES[m][1]):
            scratch += [pltpu.VMEM(whole, F32), pltpu.VMEM((6, *half), BF16), pltpu.VMEM((6, *half), BF16)]
        scratch.append(pltpu.VMEM(t.shape[2:], BF16))
    hbm = pl.BlockSpec(memory_space=pltpu.HBM)
    return pl.pallas_call(
        reduce_kernel,
        out_shape=[jax.ShapeDtypeStruct(t.shape[2:], BF16) for t in terms],
        in_specs=[hbm] * 3,
        out_specs=[hbm] * 3,
        scratch_shapes=scratch
        + [
            pltpu.SemaphoreType.DMA((REDUCE_COPIES,)),
            pltpu.SemaphoreType.DMA((REDUCE_COPIES,)),
            pltpu.SemaphoreType.DMA((6,)),
        ],
        compiler_params=pltpu.CompilerParams(collective_id=1, has_side_effects=True, vmem_limit_bytes=60 * 2**20),
        name="reduce_gradients",
    )(*terms)


def solution(mesh):
    def fetched(weights, number):
        return {name: lax.all_gather(w[number], "s", axis=0, tiled=True) for name, w in zip(NAMES, weights, strict=True)}

    def summed(term):
        return lax.psum(lax.psum_scatter(term, "s", scatter_dimension=0, tiled=True), "r")

    def step(x, dy, *weights):
        h0 = x[0]
        w0 = dict(zip(NAMES, gathered(*(w[0] for w in weights))))
        w1 = fetched(weights, 1)
        h1 = layer(h0, w0)
        _, back = jax.vjp(lambda w, h: layer(h, w), w1, h1)
        by_w1, by_h = back(dy[0])
        mine1 = [summed(by_w1[name]) for name in NAMES]
        _, back = jax.vjp(lambda w, h: layer(h, w), w0, h0)
        by_w0, by_x = back(by_h)
        mine0 = reduced([by_w0[name] for name in NAMES])
        return (by_x[None], *(jnp.stack([a, b]) for a, b in zip(mine0, mine1)))

    states, cut = P(("rep", "r", "s"), None, None), P(None, "s", None)
    return jax.shard_map(
        step,
        mesh=mesh,
        in_specs=(states, states) + (cut,) * 3,
        out_specs=(states,) + (P("rep", "s", None),) * 3,
        check_vma=False,
    )
```

time: 727 us -> 592 us (0.81)
  waiting for transfers between devices: 274 us -> 0.84 us
  Pallas kernels: 0 us -> 142 us
    pallas_call x0 -> x2, Pallas kernels: none -> 142 us  [the longest x1 83.1 us: reduced(): pl.pallas_call(reduce_kernel, out_shape=[jax.ShapeDtypeStruct(t.shape[2:]...]
    reduce_scatter x6 -> x3, waiting for transfers between devices: 108 us -> 0.02 us  [summed(): lax.psum_scatter(term, 's', scatter_dimension=0, tiled=True)]
    all_gather x6 -> x3, waiting for transfers between devices: 105 us -> 0.02 us  [fetched(): lax.all_gather(w[number], 's', axis=0, tiled=True)]
    psum x1, waiting for transfers between devices: 59.9 us -> 0.02 us  [summed(): lax.psum(lax.psum_scatter(term, 's', scatter_dimension=0, tiled=True), 'r')]
  transfers between devices with their start and end apart: 13 -> 7, of which waited for: 10 -> 0; matrix products, arithmetic and copies ran while one was open for 44% -> 57% of each run, Pallas kernels for 0% -> 24%
where the time goes in v1:
time: 592 us; the launch traced here: 584 us
  matrix products  395 us (67%)
  Pallas kernels  142 us (24%)
  local copies, waits for them, and re-layouts  18.6 us (3%)
  between operations  14.6 us (2%)
  other arithmetic  12 us (2%)
    dot_general x6, matrix products, layer(): up = jnp.dot(a, w['w_up'], preferred_element_type=jnp.float32)  141 us
    dot_general x6, matrix products, layer(): gate = jnp.dot(a, w['w_gate'], preferred_element_type=jnp.float32)  129 us
    dot_general x5, matrix products, matmul(): jnp.dot(a, w, preferred_element_type=jnp.float32).astype(jnp.bfloat16)  125 us
    pallas_call x1, Pallas kernels, reduced(): pl.pallas_call(reduce_kernel, out_shape=[jax.ShapeDtypeStruct(t.shape[2:]...  83.1 us
    pallas_call x1, Pallas kernels, gathered(): pl.pallas_call(gather_kernel, out_shape=[jax.ShapeDtypeStruct((4, 2, *w.s...  59 us
    unnamed x37, local copies, waits for them, and re-layouts  12.9 us
  transfers between devices with their start and end apart: 7, of which 0 were waited for; matrix products, arithmetic and copies ran while one was open for 57% of the time, Pallas kernels for 24%

profile of v1, /device:TPU:0, one launch (start us, length us, event | category | flops | bytes accessed | tf_op | source)
XLA Modules:
  0.0 583.6 jit_solution(12122055735183828930)
XLA Ops:
  7.2 0.0 all-gather.9.cloned.1.call-start
  7.2 2.5 fusion.68
  9.7 0.0 all-gather.9.cloned.1.call-update
  9.7 0.0 all-gather.11.cloned.1.call-start
  9.7 3.2 fusion.67
  12.9 0.0 all-gather.11.cloned.1.call-update
  13.0 0.0 all-gather.7.cloned.1.call-start
  13.0 0.7 all-gather.7.cloned.1.call-update
  13.7 0.0 reduce-scatter.4.cloned.1.call-start
  13.7 3.0 copy.10
  16.7 0.0 copy-start
  16.8 0.6 fusion.18
  17.3 0.9 copy-done.10
  18.2 59.0 %gather_weights.1 = (bf16[4,2,80,4096]{3,2,1,0:T(8,128)(2,1)}, bf16[4,2,80,4096]{3,2,1,0:T(8,128)(2,1)}, bf16[4,2,512,640]{3,2,1,0:T(8,128)(2,1)}) custom-call(bf16[80,4096]{1,0:T(8,128)(2,1)} %get-tuple-element.24.g, bf16[80,4096]{1,0:T(8,128)(2,1)} %get-tuple-element.41.u, bf16[512,640]{1,0:T(8,128)(2,1)} %get-tuple-element.26.d), custom_call_target="tpu_custom_call" | custom-call | tf_op jit(solution)/shard_map/gather_weights/pallas_call | solution.py:180
  77.2 0.0 copy-start.7
  77.2 22.3 %fusion.58 = f32[2048,4096]{1,0:T(8,128)} fusion(bf16[640,4096]{1,0:T(8,128)(2,1)} %bitcast.88, bf16[1,2048,640]{2,1,0:T(8,128)(2,1)} %param.5, f32[2048]{0:T(1024)S(1)} %fusion.60), kind=kOutput, calls=%fused_computation.76 | convolution fusion | flops 10741350400 | bytes 41426944 | tf_op jit(solution)/shard_map/dot_general | solution.py:26
  99.5 0.0 copy-done.12
  99.5 0.0 copy-done.7
  99.5 32.3 %multiply_convert_fusion.1 = (bf16[2048,4096]{1,0:T(8,128)(2,1)}, f32[2048,4096]{1,0:T(8,128)}) fusion(f32[2048,4096]{1,0:T(8,128)} %fusion.58, bf16[640,4096]{1,0:T(8,128)(2,1)} %bitcast.90, bf16[1,2048,640]{2,1,0:T(8,128)(2,1)S(1)} %copy-done.7, f32[2048]{0:T(1024)S(1)} %fusion.60), kind=kOutput, calls=%fused_computation.13 | convolution fusion | flops 10791682048 | bytes 91758592 | tf_op jit(solution)/shard_map/dot_general | solution.py:27
  131.8 4.6 copy.9
  136.4 0.0 copy-done
  136.4 17.7 %fusion.21 = (f32[2048]{0:T(1024)S(1)}, bf16[2048,640]{0,1:T(8,128)(2,1)}) fusion(bf16[2048,4096]{1,0:T(8,128)(2,1)} %get-tuple-element.29, bf16[4096,640]{1,0:T(8,128)(2,1)} %bitcast.92, bf16[1,2048,640]{1,2,0:T(8,128)(2,1)S(1)} %copy.10), kind=kOutput, calls=%fused_computation.46 | convolution fusion | flops 10743969792 | bytes 27271168 | tf_op jit(solution)/shard_map/dot_general | solution.py:15
  154.1 0.0 copy-start.5
  154.1 0.0 all-gather.9.cloned.1.call-done
  154.1 19.7 %convolution_convert_fusion.1 = bf16[2048,4096]{1,0:T(8,128)(2,1)} fusion(bf16[1,4096,640]{2,1,0:T(8,128)(2,1)} %all-gather.9.cloned.1.call-done, bf16[1,2048,640]{2,1,0:T(8,128)(2,1)} %param.6), kind=kOutput, calls=%fused_computation.22 | convolution fusion | flops 10745806848 | bytes 24641536 | tf_op jit(solution)/shard_map/transpose(jvp())/dot_general | solution.py:15
  173.8 0.0 copy-done.14
  173.8 0.0 copy-done.5
  173.8 19.9 %fusion.24 = f32[2048,4096]{1,0:T(8,128)} fusion(bf16[1,640,4096]{2,1,0:T(8,128)(2,1)} %all-gather.11.cloned.1.call-done, bf16[2048,640]{0,1:T(8,128)(2,1)S(1)} %copy-done.5, f32[2048]{0:T(1024)S(1)} %fusion.61), kind=kOutput, calls=%fused_computation.49 | convolution fusion | flops 10741350400 | bytes 41426944 | tf_op jit(solution)/shard_map/jvp()/dot_general | solution.py:27
  193.7 42.4 %fusion.1 = (bf16[2048,4096]{1,0:T(8,128)(2,1)}, f32[2048,4096]{1,0:T(8,128)}) fusion(f32[2048,4096]{1,0:T(8,128)} %fusion.24, bf16[2048,4096]{1,0:T(8,128)(2,1)} %convolution_convert_fusion.1, bf16[1,640,4096]{2,1,0:T(8,128)(2,1)} %all-gather.7.cloned.1.call-done, bf16[2048,640]{0,1:T(8,128)(2,1)S(1)} %copy-done.5, f32[2048]{0:T(1024)S(1)} %fusion.61), kind=kOutput, calls=%fused_computation.7 | convolution fusion | flops 10842013696 | bytes 108535808 | tf_op jit(solution)/shard_map/jvp()/dot_general | solution.py:26
  236.2 23.3 %fusion.13 = bf16[640,4096]{1,0:T(8,128)(2,1)} fusion(bf16[2048,4096]{1,0:T(8,128)(2,1)} %convolution_convert_fusion.1, bf16[2048,640]{0,1:T(8,128)(2,1)S(1)} %copy-done.5, f32[2048]{0:T(1024)S(1)} %fusion.61, f32[2048,4096]{1,0:T(8,128)} %get-tuple-element.34), kind=kOutput, calls=%fused_computation.36 | convolution fusion | flops 10794303488 | bytes 58204160 | tf_op jit(solution)/shard_map/transpose(jvp())/dot_general | solution.py:27
  259.5 16.1 %convolution_convert_fusion.3 = bf16[640,4096]{1,0:T(8,128)(2,1)} fusion(bf16[2048,4096]{1,0:T(8,128)(2,1)} %get-tuple-element.33, bf16[2048,640]{0,1:T(8,128)(2,1)S(1)} %copy-done.5, f32[2048]{0:T(1024)S(1)} %fusion.61), kind=kOutput, calls=%fused_computation.37 | convolution fusion | flops 10741350400 | bytes 24649728 | tf_op jit(solution)/shard_map/transpose(jvp())/dot_general | solution.py:26
  275.6 0.0 reduce-scatter.4.cloned.1.call-update
  275.6 0.0 reduce-scatter.6.cloned.1.call-start
  275.7 20.8 %fusion.36 = bf16[2048,640]{0,1:T(8,128)(2,1)S(1)} fusion(bf16[1,640,4096]{2,1,0:T(8,128)(2,1)} %all-gather.11.cloned.1.call-done, bf16[2048,4096]{1,0:T(8,128)(2,1)} %convolution_convert_fusion.1, f32[2048,4096]{1,0:T(8,128)} %get-tuple-element.34), kind=kOutput, calls=%fused_computation.60 | convolution fusion | flops 10789060608 | bytes 58195968 | tf_op jit(solution)/shard_map/transpose(jvp())/dot_general | solution.py:27
  296.5 0.0 copy-start.15
  296.5 0.0 copy-start.4
  296.5 0.0 copy-start.6
  296.5 16.5 %fusion.23 = (f32[2048]{0:T(1024)S(1)}, bf16[2048,640]{0,1:T(8,128)(2,1)S(1)}) fusion(bf16[2048,640]{0,1:T(8,128)(2,1)S(1)} %copy-done.5, bf16[2048,640]{0,1:T(8,128)(2,1)S(1)} %fusion.36, bf16[2048,4096]{1,0:T(8,128)(2,1)} %get-tuple-element.33, bf16[1,640,4096]{2,1,0:T(8,128)(2,1)} %all-gather.7.cloned.1.call-done), kind=kOutput, calls=%fused_computation.48 | convolution fusion | flops 10743969792 | bytes 29892608 | tf_op jit(solution)/shard_map/transpose(jvp())/dot_general | solution.py:26
  313.0 0.0 copy-done.15
  313.1 0.0 copy-done.4
  313.1 0.0 copy-done.6
  313.1 1.9 fusion.47
  315.0 39.2 %fusion.3 = (bf16[2048,4096]{1,0:T(8,128)(2,1)}, bf16[2048,4096]{1,0:T(8,128)(2,1)}) fusion(f32[2048,4096]{1,0:T(8,128)} %fusion.58, f32[2048,4096]{1,0:T(8,128)} %get-tuple-element.30, bf16[2048,640]{0,1:T(8,128)(2,1)S(1)} %fusion.47, bf16[4096,640]{1,0:T(8,128)(2,1)} %bitcast.93), kind=kOutput, calls=%fused_computation.9 | convolution fusion | flops 10846470144 | bytes 108527616 | tf_op jit(solution)/shard_map/transpose(jvp())/dot_general | solution.py:15
  354.2 0.0 copy-done.2
  354.2 0.0 reduce-scatter.6.cloned.1.call-update
  354.2 0.0 reduce-scatter.8.cloned.1.call-start
  354.3 21.7 %fusion.35 = bf16[2048,640]{0,1:T(8,128)(2,1)S(1)} fusion(bf16[640,4096]{1,0:T(8,128)(2,1)} %bitcast.91, bf16[2048,4096]{1,0:T(8,128)(2,1)} %get-tuple-element.38, f32[2048,4096]{1,0:T(8,128)} %fusion.58), kind=kOutput, calls=%fused_computation.59 | convolution fusion | flops 10789060608 | bytes 58195968 | tf_op jit(solution)/shard_map/transpose(jvp())/dot_general | solution.py:27
  376.0 15.0 %fusion.19 = (f32[2048]{0:T(1024)S(1)}, bf16[2048,640]{0,1:T(8,128)(2,1)S(1)}) fusion(bf16[1,2048,640]{1,2,0:T(8,128)(2,1)S(1)} %copy-done.1, bf16[2048,640]{0,1:T(8,128)(2,1)S(1)} %fusion.35, bf16[2048,4096]{1,0:T(8,128)(2,1)} %get-tuple-element.37, bf16[640,4096]{1,0:T(8,128)(2,1)S(1)} %bitcast.89), kind=kOutput, calls=%fused_computation.44 | convolution fusion | flops 10743969792 | bytes 29892608 | tf_op jit(solution)/shard_map/transpose(jvp())/dot_general | solution.py:26
  391.1 3.4 fusion.46
  394.4 4.4 copy.11
  398.8 28.9 %fusion.11 = bf16[4096,640]{1,0:T(8,128)(2,1)} fusion(f32[2048,4096]{1,0:T(8,128)} %fusion.24, bf16[1,2048,640]{2,1,0:T(8,128)(2,1)} %param.6, f32[2048,4096]{1,0:T(8,128)} %get-tuple-element.34), kind=kOutput, calls=%fused_computation.34 | convolution fusion | flops 10790371328 | bytes 74973184 | tf_op jit(solution)/shard_map/transpose(jvp())/dot_general | solution.py:15
  427.8 0.0 reduce-scatter.8.cloned.1.call-update
  427.8 0.0 all-reduce.3.cloned.1.call-start
  427.8 16.3 %convolution_convert_fusion.4 = bf16[640,4096]{1,0:T(8,128)(2,1)} fusion(bf16[2048,4096]{1,0:T(8,128)(2,1)} %get-tuple-element.37, bf16[1,2048,640]{1,2,0:T(8,128)(2,1)S(1)} %copy-done.1, f32[2048]{0:T(1024)S(1)} %copy-done.13), kind=kOutput, calls=%fused_computation.38 | convolution fusion | flops 10741350400 | bytes 24649728 | tf_op jit(solution)/shard_map/transpose(jvp())/dot_general | solution.py:26
  444.2 23.0 %fusion.12 = bf16[640,4096]{1,0:T(8,128)(2,1)} fusion(bf16[2048,4096]{1,0:T(8,128)(2,1)} %get-tuple-element.38, bf16[1,2048,640]{1,2,0:T(8,128)(2,1)S(1)} %copy-done.1, f32[2048]{0:T(1024)S(1)} %copy-done.13, f32[2048,4096]{1,0:T(8,128)} %fusion.58), kind=kOutput, calls=%fused_computation.35 | convolution fusion | flops 10794303488 | bytes 58204160 | tf_op jit(solution)/shard_map/transpose(jvp())/dot_general | solution.py:27
  467.2 0.0 reduce-scatter.8.cloned.1.call-done
  467.2 0.0 all-reduce.3.cloned.1.call-update
  467.2 20.0 %convolution_convert_fusion.2 = bf16[4096,640]{1,0:T(8,128)(2,1)} fusion(bf16[2048,4096]{1,0:T(8,128)(2,1)} %get-tuple-element.29, bf16[2048,640]{0,1:T(8,128)(2,1)} %copy-done.2), kind=kOutput, calls=%fused_computation.33 | convolution fusion | flops 10740039680 | bytes 24641536 | tf_op jit(solution)/shard_map/transpose(jvp())/dot_general | solution.py:15
  487.2 83.1 %reduce_gradients.1 = (bf16[80,4096]{1,0:T(8,128)(2,1)}, bf16[80,4096]{1,0:T(8,128)(2,1)}, bf16[512,640]{1,0:T(8,128)(2,1)}) custom-call(bf16[4,2,80,4096]{3,2,1,0:T(8,128)(2,1)} %bitcast.79, bf16[4,2,80,4096]{3,2,1,0:T(8,128)(2,1)} %bitcast.80, bf16[4,2,512,640]{3,2,1,0:T(8,128)(2,1)} %bitcast.81), custom_call_target="tpu_custom_call" | custom-call | tf_op jit(solution)/shard_map/reduce_gradients/pallas_call | solution.py:391
  570.3 0.0 all-reduce.3.cloned.1.call-done
  570.3 2.6 pad_maximum_fusion
  572.9 2.5 pad_maximum_fusion.1
  575.3 0.0 copy-done.8
  575.3 1.2 pad_maximum_fusion.2
  (25 shorter events, 0.1 us)
Async XLA Ops:
  7.2 146.9 %all-gather.9.cloned.1.call-start = ((), (), s32[]{:S(2)}) async-start(), calls=%async_computation.7 | async-start | bytes 5898240 | tf_op jit(solution)/shard_map/all_gather | solution.py:409
  9.7 164.1 %all-gather.11.cloned.1.call-start = ((), (), s32[]{:S(2)}) async-start(), calls=%async_computation.8 | async-start | bytes 5898240 | tf_op jit(solution)/shard_map/all_gather | solution.py:409
  13.0 180.8 %all-gather.7.cloned.1.call-start = ((), (), s32[]{:S(2)}) async-start(), calls=%async_computation.6 | async-start | bytes 5898240 | tf_op jit(solution)/shard_map/all_gather | solution.py:409
  13.7 453.5 %reduce-scatter.4.cloned.1.call-start = ((), (), s32[]{:S(2)}) async-start(), calls=%async_computation.3 | async-start | bytes 5898240 | tf_op jit(solution)/shard_map/reduce_scatter | solution.py:412
  16.7 119.6 %copy-start = (bf16[1,2048,640]{1,2,0:T(8,128)(2,1)}, bf16[1,2048,640]{1,2,0:T(8,128)(2,1)S(1)}, u32[]{:S(2)}) copy-start(bf16[1,2048,640]{1,2,0:T(8,128)(2,1)S(1)} %copy.10) | copy-start | bytes 7864324
  17.3 0.9 copy-start.10
  18.2 81.2 %copy-start.12 = (f32[2048]{0:T(1024)}, f32[2048]{0:T(1024)S(1)}, u32[]{:S(2)}) copy-start(f32[2048]{0:T(1024)S(1)} %fusion.60) | copy-start | bytes 24580
  77.2 22.3 %copy-start.7 = (bf16[1,2048,640]{2,1,0:T(8,128)(2,1)S(1)}, bf16[1,2048,640]{2,1,0:T(8,128)(2,1)}, u32[]{:S(2)}) copy-start(bf16[1,2048,640]{2,1,0:T(8,128)(2,1)} %param.5) | copy-start | bytes 7864324
  154.0 19.8 %copy-start.14 = (f32[2048]{0:T(1024)}, f32[2048]{0:T(1024)S(1)}, u32[]{:S(2)}) copy-start(f32[2048]{0:T(1024)S(1)} %get-tuple-element.31) | copy-start | bytes 24580
  154.1 19.8 %copy-start.5 = (bf16[2048,640]{0,1:T(8,128)(2,1)S(1)}, bf16[2048,640]{0,1:T(8,128)(2,1)}, u32[]{:S(2)}) copy-start(bf16[2048,640]{0,1:T(8,128)(2,1)} %get-tuple-element.32) | copy-start | bytes 7864324
  275.6 191.5 %reduce-scatter.6.cloned.1.call-start = ((), (), s32[]{:S(2)}) async-start(), calls=%async_computation.4 | async-start | bytes 5898240 | tf_op jit(solution)/shard_map/reduce_scatter | solution.py:412
  296.5 16.6 %copy-start.15 = (f32[2048]{0:T(1024)S(1)}, f32[2048]{0:T(1024)}, u32[]{:S(2)}) copy-start(f32[2048]{0:T(1024)} %copy-done.14) | copy-start | bytes 24580
  296.5 16.6 %copy-start.4 = (bf16[1,2048,640]{1,2,0:T(8,128)(2,1)S(1)}, bf16[1,2048,640]{1,2,0:T(8,128)(2,1)}, u32[]{:S(2)}) copy-start(bf16[1,2048,640]{1,2,0:T(8,128)(2,1)} %copy.9) | copy-start | bytes 7864324
  296.5 16.6 %copy-start.6 = (bf16[2048,640]{0,1:T(8,128)(2,1)S(1)}, bf16[2048,640]{0,1:T(8,128)(2,1)}, u32[]{:S(2)}) copy-start(bf16[2048,640]{0,1:T(8,128)(2,1)} %get-tuple-element.32) | copy-start | bytes 7864324
  315.0 39.2 %copy-start.2 = (bf16[2048,640]{0,1:T(8,128)(2,1)}, bf16[2048,640]{0,1:T(8,128)(2,1)S(1)}, u32[]{:S(2)}) copy-start(bf16[2048,640]{0,1:T(8,128)(2,1)S(1)} %fusion.47) | copy-start | bytes 7864324
  354.2 113.0 %reduce-scatter.8.cloned.1.call-start = ((), (), s32[]{:S(2)}) async-start(), calls=%async_computation.5 | async-start | bytes 5898240 | tf_op jit(solution)/shard_map/reduce_scatter | solution.py:412
  354.2 21.7 %copy-start.1 = (bf16[1,2048,640]{1,2,0:T(8,128)(2,1)S(1)}, bf16[1,2048,640]{1,2,0:T(8,128)(2,1)}, u32[]{:S(2)}) copy-start(bf16[1,2048,640]{1,2,0:T(8,128)(2,1)} %copy-done) | copy-start | bytes 7864324
  354.3 21.7 %copy-start.16 = (bf16[4,2,80,4096]{3,2,1,0:T(8,128)(2,1)S(1)}, bf16[4,2,80,4096]{3,2,1,0:T(8,128)(2,1)}, u32[]{:S(2)}) copy-start(bf16[4,2,80,4096]{3,2,1,0:T(8,128)(2,1)} %get-tuple-element.10) | copy-start | bytes 15728644
  376.0 15.1 %copy-start.11 = (f32[2048]{0:T(1024)S(1)}, f32[2048]{0:T(1024)}, u32[]{:S(2)}) copy-start(f32[2048]{0:T(1024)} %copy-done.10) | copy-start | bytes 24580
  376.0 15.1 %copy-start.3 = (bf16[2048,640]{0,1:T(8,128)(2,1)S(1)}, bf16[2048,640]{0,1:T(8,128)(2,1)}, u32[]{:S(2)}) copy-start(bf16[2048,640]{0,1:T(8,128)(2,1)} %copy-done.2) | copy-start | bytes 7864324
  376.0 15.1 %copy-start.13 = (f32[2048]{0:T(1024)S(1)}, f32[2048]{0:T(1024)}, u32[]{:S(2)}) copy-start(f32[2048]{0:T(1024)} %copy-done.12) | copy-start | bytes 24580
  427.8 142.5 %all-reduce.3.cloned.1.call-start = ((), (), s32[]{:S(2)}) async-start(), calls=%async_computation.9 | async-start | bytes 3932160 | tf_op jit(solution)/shard_map/psum | solution.py:412
  570.3 5.1 copy-start.9
  570.3 5.0 copy-start.8
Sparse Core Ops, SparseCore 0:
  9.8 54.6 all-gather.8
  66.2 35.3 all-gather.10
  103.8 36.2 all-gather.6
  275.8 37.0 reduce-scatter.3
  354.3 37.0 reduce-scatter.5
  427.9 37.0 reduce-scatter.7
  468.8 93.8 all-reduce.2

commit v2 on v0

v2 whole, which is shorter than its diff:
```python
import functools

import jax
import jax.numpy as jnp
from jax import lax
from jax.experimental import pallas as pl
from jax.experimental.pallas import tpu as pltpu
from jax.sharding import PartitionSpec as P

F32, BF16 = jnp.float32, jnp.bfloat16
MESH = pl.DeviceIdType.MESH


class Place:
    def __init__(self):
        rep, r, s = lax.axis_index("rep"), lax.axis_index("r"), lax.axis_index("s")
        self.c = s % 2
        at = {"x": s // 2, "y": r // 4, "z": r % 4}
        self.step = {a: [(at[a] + k) % 4 for k in range(4)] for a in "xyz"}

        def device(c, x, y, z):
            return (rep, y * 4 + z, x * 2 + c)

        self.other = device(1 - self.c, **at)
        self.who = {(a, k): device(self.c, **{**at, a: self.step[a][k]}) for a in "xyz" for k in (1, 2, 3)}

    def barrier(self):
        semaphore = pltpu.get_barrier_semaphore()
        for who in [self.other] + [self.who[a, k] for a in "xyz" for k in (1, 2, 3)]:
            pl.semaphore_signal(semaphore, inc=1, device_id=who, device_id_type=MESH)
        pl.semaphore_wait(semaphore, 10)


class Copy:
    def __init__(self, make):
        self.make = make

    def start(self):
        self.make().start()

    def wait(self):
        self.make().wait()

    def wait_recv(self):
        self.make().wait_recv()

    def wait_send(self):
        self.make().wait_send()


class Sender:
    def __init__(self, send, recv):
        self.send, self.recv, self.made = send, recv, []

    def copy(self, ends, who):
        k = len(self.made)

        def make():
            src, dst = ends()
            return pltpu.make_async_remote_copy(
                src_ref=src,
                dst_ref=dst,
                send_sem=self.send.at[k],
                recv_sem=self.recv.at[k],
                device_id=who,
                device_id_type=MESH,
            )

        self.made.append(Copy(make))
        return self.made[-1]

    def finish(self):
        for made in self.made:
            made.wait_send()


def run(phases, slots, position):
    for phase, (step, place) in zip(phases, slots, strict=True):
        if place == position:
            pl.when(pl.program_id(0) == step)(phase)


class Part:
    def __init__(self, own, out, axis, dim, base, size):
        self.own, self.out, self.axis, self.dim, self.base, self.size = own, out, axis, dim, base, size

    def cut(self, q, half):
        w = self.size // 4
        start = self.base + q * w
        if half is not None:
            w //= 2
            start = start + half * w
        return pl.ds(pl.multiple_of(start, w), w)

    def mine(self, q):
        d = self.cut(q, None)
        return self.own.at[:, d] if self.dim else self.own.at[d]

    def there(self, x, c, q, half=None):
        d = self.cut(q, half)
        return self.out.at[x, c, :, d] if self.dim else self.out.at[x, c, d]


GATHER_COPIES = 3 + 4 * 31


def gathering(me, go, owns, outs, local):
    c, other, who = me.c, me.other, me.who
    x, x1, x2, x3 = me.step["x"]
    (g, u, d), (og, ou, od) = owns, outs
    columns, rows = g.shape[1], d.shape[0]
    parts = [
        Part(g, og, "y", 1, 0, columns // 2),
        Part(g, og, "z", 1, columns // 2, columns // 2),
        Part(u, ou, "y", 1, 0, columns),
        Part(d, od, "z", 0, 0, rows),
    ]

    def own(i):
        return Copy(lambda: pltpu.make_async_copy(owns[i], outs[i].at[x, c], local.at[i]))

    def swap(i):
        return go.copy(lambda: (owns[i], outs[i].at[x, c]), other)

    def first(p, k):
        q = me.step[p.axis][0]
        return go.copy(lambda: (p.mine(q), p.there(x, c, q)), who["x", k])

    def on(p, at, q, half, to):
        return go.copy(lambda: (p.there(at, c, q, half), p.there(at, c, q, half)), to)

    here, swaps = [own(i) for i in range(3)], [swap(i) for i in range(3)]
    plans = []
    for p in parts:
        q, q1, q2, q3 = me.step[p.axis]
        up, down = who[p.axis, 1], who[p.axis, 3]
        plans.append(
            dict(
                first=[first(p, 1), first(p, 3)],
                second=[on(p, x3, q, 0, who["x", 1]), on(p, x1, q, 1, who["x", 3])],
                along=[[on(p, at, q, None, to) for to in (up, down)] for at in (x3, x1, x2)],
                across=[on(p, at, q, None, other) for at in (x3, x1, x2)],
                last=[[on(p, at, q3, 0, up), on(p, at, q1, 1, down)] for at in (x3, x1, x2)],
                across1=[[on(p, at, q3, None, other), on(p, at, q1, None, other)] for at in (x3, x1, x2)],
                across2=[[on(p, at, q2, half, other) for half in (0, 1)] for at in (x3, x1, x2)],
            )
        )

    def start():
        for i in here:
            i.start()
        me.barrier()
        for t in plans:
            for i in t["first"]:
                i.start()
        for i in swaps:
            i.start()

    def hand_on():
        for t in plans:
            for k in (0, 1):
                t["first"][k].wait_recv()
                t["second"][k].start()
                for i in t["along"][k]:
                    i.start()
                t["across"][k].start()

    def far():
        for t in plans:
            for i in t["second"]:
                i.wait_recv()
            for i in t["along"][2]:
                i.start()
            t["across"][2].start()

    def turn(k):
        def phase():
            for t in plans:
                for j in (0, 1):
                    t["along"][k][j].wait_recv()
                    t["last"][k][j].start()
                    t["across1"][k][j].start()

        return phase

    def ends(ks):
        def phase():
            for k in ks:
                for t in plans:
                    for j in (0, 1):
                        t["last"][k][j].wait_recv()
                        t["across2"][k][j].start()

        return phase

    def finish():
        for i in swaps:
            i.wait_recv()
        for t in plans:
            for i in t["across"] + sum(t["across1"] + t["across2"], []):
                i.wait_recv()
        for i in here:
            i.wait()
        go.finish()

    return [start, hand_on, far, turn(0), turn(1), turn(2), ends((0, 1, 2)), finish]


GATHER_SCRATCH = [
    pltpu.SemaphoreType.DMA((GATHER_COPIES,)),
    pltpu.SemaphoreType.DMA((GATHER_COPIES,)),
    pltpu.SemaphoreType.DMA((3,)),
]
HBM = pl.BlockSpec(memory_space=pltpu.HBM)


def rows_of(w, layer):
    return pl.BlockSpec((1, *w.shape[1:]), lambda *_: (layer, 0, 0), pipeline_mode=pl.Buffered(1))


def whole_shapes(weights):
    return [jax.ShapeDtypeStruct((4, 2, *w.shape[1:]), w.dtype) for w in weights]


def flat(ws):
    return [w.reshape(8 * w.shape[2], w.shape[3]) for w in ws]


def gather_kernel(g, u, d, og, ou, od, send, recv, local):
    for phase in gathering(Place(), Sender(send, recv), [w.at[0] for w in (g, u, d)], (og, ou, od), local):
        phase()


def gathered(weights, layer):
    return flat(
        pl.pallas_call(
            gather_kernel,
            grid=(1,),
            out_shape=whole_shapes(weights),
            in_specs=[rows_of(w, layer) for w in weights],
            out_specs=[HBM] * 3,
            scratch_shapes=GATHER_SCRATCH,
            compiler_params=pltpu.CompilerParams(collective_id=0, has_side_effects=True),
            name="gather_weights",
        )(*weights)
    )


def added(dst, *srcs):
    shape = dst.shape
    if len(shape) == 3:
        for i in range(shape[0]):
            added(dst.at[i], *(s.at[i] for s in srcs))
        return
    rows, columns = shape
    step = 16 if rows % 16 == 0 else rows
    wide = min(columns, 1024)

    @pl.loop(0, rows // step)
    def _(i):
        for j in range(0, columns, wide):
            at = (pl.ds(pl.multiple_of(i * step, step), step), pl.ds(j, min(wide, columns - j)))
            total = srcs[0][at].astype(F32)
            for s in srcs[1:]:
                total = total + s[at].astype(F32)
            dst[at] = total.astype(dst.dtype)


class Ring:
    def __init__(self, me, go, axis, terms, cut, out, got, hold):
        self.terms, self.cut, self.out, self.got = terms, cut, out, got
        self.at = me.step[axis]
        up, down = me.who[axis, 1], me.who[axis, 3]

        def slot(k, piece, half, to):
            def src():
                return cut(terms[1], self.at[piece], half) if hold is None else hold.at[k]

            return src, piece, half, go.copy(lambda: (src(), got.at[k]), to)

        self.slots = [
            slot(0, 2, 0, up),
            slot(1, 2, 1, down),
            slot(2, 1, 1, up),
            slot(3, 3, 0, down),
            slot(4, 1, 0, up),
            slot(5, 3, 1, down),
        ]

    def term(self, piece, half):
        return [self.cut(t, self.at[piece], half) for t in self.terms]

    def send(self, k, *more):
        src, piece, half, copy = self.slots[k]
        added(src(), *self.term(piece, half), *more)
        copy.start()

    def start(self):
        for k in range(4):
            self.send(k)

    def middle(self):
        for k in (0, 1):
            self.slots[k][3].wait_recv()
            self.send(4 + k, self.got.at[k])

    def end(self, cut_out):
        for k in (2, 3, 4, 5):
            self.slots[k][3].wait_recv()
        added(cut_out(self.out, 0), *self.term(0, 0), self.got.at[3], self.got.at[4])
        added(cut_out(self.out, 1), *self.term(0, 1), self.got.at[2], self.got.at[5])


def piece(dim, n):
    def cut(ref, q, half):
        w = ref.shape[dim] // 4
        at = [slice(None)] * len(ref.shape)
        if n == dim:
            at[dim] = pl.ds(pl.multiple_of(q * w + half * (w // 2), w // 2), w // 2)
        else:
            at[dim] = pl.ds(pl.multiple_of(q * w, w), w)
            h = ref.shape[n] // 2
            at[n] = pl.ds(half * h, h)
        if dim == 0 and len(ref.shape) == 3:
            at[0] = q
        return ref.at[tuple(at)]

    return cut


def halves(n):
    def cut(ref, half):
        h = ref.shape[n] // 2
        at = [slice(None)] * len(ref.shape)
        at[n] = pl.ds(half * h, h)
        return ref.at[tuple(at)]

    return cut


ROUTES = (
    (1, (("x", 0, 2), ("y", 1, 1), ("z", 1, 1))),
    (1, (("y", 2, 0), ("z", 2, 0), ("x", 0, 2))),
    (0, (("z", 1, 0), ("x", 0, 1), ("y", 0, 0))),
)


def plan(shape, steps):
    sizes = []
    for _, dim, n in steps:
        cut = list(shape)
        if dim == 0 and len(cut) == 3:
            cut = cut[1:]
            whole = list(cut)
            cut[n - 1] //= 2
        else:
            cut[dim] //= 4
            whole = list(cut)
            cut[n] //= 2
        sizes.append((tuple(cut), tuple(whole)))
        shape = tuple(whole)
    return sizes


REDUCE_COPIES = 3 * (1 + 18 + 3 + 4)


def reducing(me, go, terms, outs, scratch, local):
    c = me.c
    per = len(scratch) // 3
    bufs = [scratch[m * per : (m + 1) * per] for m in range(3)]

    def own(m):
        return Copy(lambda: pltpu.make_async_copy(terms[m].at[:, c], bufs[m][0], local.at[m]))

    def swap(m):
        return go.copy(lambda: (terms[m].at[:, 1 - c], bufs[m][1]), me.other)

    here, swaps = [own(m) for m in range(3)], [swap(m) for m in range(3)]
    rings = []
    for m in range(3):
        b, (_, steps) = bufs[m], ROUTES[m]
        made = []
        for k, (axis, dim, n) in enumerate(steps):
            t = (b[0], b[1]) if k == 0 else (made[-1].out,)
            at = 2 if k == 0 else 4 + 3 * (k - 1)
            made.append(Ring(me, go, axis, t, piece(dim, n), b[at], b[at + 1], None if k == 0 else b[at + 2]))
            made[-1].halves = halves(n - 1 if dim == 0 and len(t[0].shape) == 3 else n)
        rings.append(made)

    spread = []
    for m in range(3):
        dim, done = ROUTES[m][0], bufs[m][-1]
        size = done.shape[dim] // 16
        high, low = ("z", "y") if m == 2 else ("y", "z")

        def at(hi, lo=None, half=None, done=done, dim=dim, size=size):
            w = size if lo is not None else 4 * size
            start = hi * (4 * size) + (lo * size if lo is not None else 0)
            if half is not None:
                w //= 2
                start = start + half * w
            d = pl.ds(pl.multiple_of(start, w), w)
            return done.at[:, d] if dim else done.at[d]

        def copy(to, *where, at=at):
            return go.copy(lambda: (at(*where), at(*where)), to)

        h, h1, _, h3 = me.step[high]
        l = me.step[low][0]
        spread.append(
            dict(
                mine=lambda at=at, h=h, l=l: at(h, l),
                low=[copy(me.who[low, k], h, l) for k in (1, 2, 3)],
                near=[copy(me.who[high, 1], h), copy(me.who[high, 3], h)],
                far=[copy(me.who[high, 1], h3, None, 0), copy(me.who[high, 3], h1, None, 1)],
            )
        )
    back = [
        Copy(lambda m=m: pltpu.make_async_copy(bufs[m][-1], outs[m], local.at[3 + m])) for m in range(3)
    ]

    def start():
        for i in here:
            i.start()
        me.barrier()
        for i in swaps:
            i.start()

    def first(m):
        def phase():
            here[m].wait()
            swaps[m].wait_recv()
            rings[m][0].start()

        return phase

    def middle(k):
        def phase():
            for r in rings:
                r[k].middle()

        return phase

    def end(k):
        def phase():
            for r in rings:
                r[k].end(r[k].halves)
                if k < 2:
                    r[k + 1].start()

        return phase

    def low():
        end(2)()
        for m, t in enumerate(spread):
            added(t["mine"](), rings[m][2].out)
            for i in t["low"]:
                i.start()

    def near():
        for t in spread:
            for i in t["low"]:
                i.wait_recv()
            for i in t["near"]:
                i.start()

    def far():
        for k in (0, 1):
            for t in spread:
                t["near"][k].wait_recv()
                t["far"][k].start()

    def finish():
        for m, t in enumerate(spread):
            for i in t["far"]:
                i.wait_recv()
            back[m].start()
        for i in back:
            i.wait()
        go.finish()

    return [start, first(0), first(1), first(2), middle(0), end(0), middle(1), end(1), middle(2), low, near, far, finish]


def reduce_scratch(shapes):
    scratch = []
    for m, s in enumerate(shapes):
        block = (4, *s[2:])
        scratch += [pltpu.VMEM(block, BF16)] * 2
        for k, (half, whole) in enumerate(plan(block, ROUTES[m][1])):
            scratch += [pltpu.VMEM(whole, F32), pltpu.VMEM((6, *half), BF16)]
            if k:
                scratch.append(pltpu.VMEM((6, *half), BF16))
        scratch.append(pltpu.VMEM(s[2:], BF16))
    return scratch + [
        pltpu.SemaphoreType.DMA((REDUCE_COPIES,)),
        pltpu.SemaphoreType.DMA((REDUCE_COPIES,)),
        pltpu.SemaphoreType.DMA((6,)),
    ]


def blocks_of(terms):
    return [t.reshape(4, 2, t.shape[0] // 8, t.shape[1]) for t in terms]


def reduce_kernel(*refs):
    terms, outs, scratch = refs[:3], refs[3:6], refs[6:]
    send, recv, local = scratch[-3:]
    for phase in reducing(Place(), Sender(send, recv), terms, outs, scratch[:-3], local):
        phase()


def reduced(terms):
    terms = blocks_of(terms)
    return pl.pallas_call(
        reduce_kernel,
        out_shape=[jax.ShapeDtypeStruct(t.shape[2:], BF16) for t in terms],
        in_specs=[HBM] * 3,
        out_specs=[HBM] * 3,
        scratch_shapes=reduce_scratch([t.shape for t in terms]),
        compiler_params=pltpu.CompilerParams(collective_id=1, has_side_effects=True, vmem_limit_bytes=60 * 2**20),
        name="reduce_gradients",
    )(*terms)


def dot(a, b):
    return jnp.dot(a, b, preferred_element_type=F32)


def scale_of(wide):
    return lax.rsqrt(jnp.mean(wide * wide, -1, keepdims=True) + 1e-6)


def by_rows(tokens):
    def loop(body):
        @pl.loop(0, tokens // 256)
        def _(t):
            body(pl.ds(pl.multiple_of(t * 256, 256), 256))

    return loop


def dh_rows(h, dy, da, at):
    wide = h[at, :].astype(F32)
    scale = scale_of(wide)
    by_a = da[at, :].astype(BF16).astype(F32)
    inner = jnp.mean(by_a * wide, -1, keepdims=True)
    by_h = (by_a * scale - wide * (scale * scale * scale * inner)).astype(BF16)
    return dy[at, :] + by_h


FORWARD_SLOTS = ((0, 0), (2, 0), (3, 0), (3, 1), (4, 1), (5, 1), (6, 1), (7, 2))


def forward_kernel(tile, h, wg, wu, wd, ng, nu, nd, g_out, u_out, h_out, og, ou, od, a, acc, send, recv, local):
    i, n = pl.program_id(0), pl.num_programs(0)
    tokens = h.shape[0]
    phases = gathering(Place(), Sender(send, recv), [w.at[0] for w in (ng, nu, nd)], (og, ou, od), local)
    run(phases, FORWARD_SLOTS, 0)

    @pl.when(i == 0)
    def _():
        @by_rows(tokens)
        def _(at):
            wide = h[at, :].astype(F32)
            a[at, :] = (wide * scale_of(wide)).astype(BF16)
            acc[at, :] = jnp.zeros((256, h.shape[1]), F32)

    for t in range(tokens // tile):
        if t:
            run(phases, FORWARD_SLOTS, t)
        at = pl.ds(t * tile, tile)
        g = dot(a[at, :], wg[...])
        u = dot(a[at, :], wu[...])
        g_out[at, :] = g
        u_out[at, :] = u
        mid = (g * jax.nn.sigmoid(g) * u).astype(BF16)
        acc[at, :] += dot(mid, wd[...])

    @pl.when(i == n - 1)
    def _():
        @by_rows(tokens)
        def _(at):
            h_out[at, :] = h[at, :] + acc[at, :].astype(BF16)

    run(phases, FORWARD_SLOTS, 2)


def specs(tokens, d, chunk):
    whole = pl.BlockSpec((tokens, d), lambda i: (0, 0), pipeline_mode=pl.Buffered(1))
    across = pl.BlockSpec((d, chunk), lambda i: (0, i))
    down = pl.BlockSpec((chunk, d), lambda i: (i, 0))
    wide = pl.BlockSpec((tokens, chunk), lambda i: (0, i))
    return whole, across, down, wide


def first_of(tokens, d):
    return pl.BlockSpec((None, tokens, d), lambda i: (0, 0, 0), pipeline_mode=pl.Buffered(1))


def forward(x, w, weights, layer, chunk=512, tile=1024):
    _, tokens, d = x.shape
    ff = w[0].shape[1]
    whole, across, down, wide = specs(tokens, d, chunk)
    out = pl.pallas_call(
        functools.partial(forward_kernel, tile),
        grid=(ff // chunk,),
        out_shape=[jax.ShapeDtypeStruct((tokens, ff), F32)] * 2
        + [jax.ShapeDtypeStruct((tokens, d), BF16)]
        + whole_shapes(weights),
        in_specs=[first_of(tokens, d), across, across, down] + [rows_of(v, layer) for v in weights],
        out_specs=[wide, wide, whole] + [HBM] * 3,
        scratch_shapes=[pltpu.VMEM((tokens, d), BF16), pltpu.VMEM((tokens, d), F32)] + GATHER_SCRATCH,
        compiler_params=pltpu.CompilerParams(collective_id=1, has_side_effects=True, vmem_limit_bytes=60 * 2**20),
        name="forward_layer",
    )(x, *w, *weights)
    return out[0], out[1], out[2], flat(out[3:])


def backward_kernel(tile, h, dy, wg, wu, wd, dwg, dwu, dwd, dh, a, at_, dyt, da, mid, dg, du):
    i, n = pl.program_id(0), pl.num_programs(0)
    tokens = h.shape[0]

    @pl.when(i == 0)
    def _():
        @by_rows(tokens)
        def _(at):
            wide = h[at, :].astype(F32)
            rows = (wide * scale_of(wide)).astype(BF16)
            a[at, :] = rows
            at_[:, at] = rows.T
            dyt[:, at] = dy[at, :].T
            da[at, :] = jnp.zeros((256, h.shape[1]), F32)

    wdt, wgt, wut = wd[...].T, wg[...].T, wu[...].T
    for t in range(tokens // tile):
        at = pl.ds(t * tile, tile)
        g = dot(a[at, :], wg[...])
        u = dot(a[at, :], wu[...])
        dm = dot(dy[at, :], wdt).astype(BF16).astype(F32)
        sg = jax.nn.sigmoid(g)
        s = g * sg
        mid[at, :] = (s * u).astype(BF16)
        dub = (dm * s).astype(BF16)
        dgb = (dm * u * (sg + s * (1.0 - sg))).astype(BF16)
        du[at, :] = dub
        dg[at, :] = dgb
        da[at, :] += dot(dgb, wgt) + dot(dub, wut)
    dwg[...] = dot(at_[...], dg[...]).astype(BF16)
    dwu[...] = dot(at_[...], du[...]).astype(BF16)
    dwd[...] = dot(dyt[...], mid[...]).T.astype(BF16)

    @pl.when(i == n - 1)
    def _():
        @by_rows(tokens)
        def _(at):
            dh[at, :] = dh_rows(h, dy, da, at)


def backward(h, dy, w, chunk=512, tile=1024):
    tokens, d = h.shape
    ff = w[0].shape[1]
    whole, across, down, wide = specs(tokens, d, chunk)
    return pl.pallas_call(
        functools.partial(backward_kernel, tile),
        grid=(ff // chunk,),
        out_shape=[jax.ShapeDtypeStruct((d, ff), BF16)] * 2
        + [jax.ShapeDtypeStruct((ff, d), BF16), jax.ShapeDtypeStruct((tokens, d), BF16)],
        in_specs=[whole, first_of(tokens, d), across, across, down],
        out_specs=[across, across, down, whole],
        scratch_shapes=[
            pltpu.VMEM((tokens, d), BF16),
            pltpu.VMEM((d, tokens), BF16),
            pltpu.VMEM((d, tokens), BF16),
            pltpu.VMEM((tokens, d), F32),
        ]
        + [pltpu.VMEM((tokens, chunk), BF16)] * 3,
        compiler_params=pltpu.CompilerParams(vmem_limit_bytes=62 * 2**20),
        name="backward_layer",
    )(h, dy, *w)


WEIGHTS_SLOTS = (
    ((0, 0), (2, 0), (3, 0), (4, 0), (5, 0), (7, 0), (8, 0), (9, 0), (10, 0), (11, 0), (12, 0), (13, 0), (15, 2))
)


def weights_kernel(tile, h, dy, wd, g, u, t0, t1, t2, dwg, dwu, dwd, dg, du, o0, o1, o2, at_, dyt, mid, *scratch):
    i = pl.program_id(0)
    tokens = h.shape[0]
    send, recv, local = scratch[-3:]
    phases = reducing(Place(), Sender(send, recv), (t0, t1, t2), (o0, o1, o2), scratch[:-3], local)
    run(phases, WEIGHTS_SLOTS, 0)

    @pl.when(i == 0)
    def _():
        @by_rows(tokens)
        def _(at):
            wide = h[at, :].astype(F32)
            at_[:, at] = (wide * scale_of(wide)).astype(BF16).T
            dyt[:, at] = dy[at, :].T

    wdt = wd[...].T
    for t in range(tokens // tile):
        at = pl.ds(t * tile, tile)
        gg, uu = g[at, :], u[at, :]
        dm = dot(dy[at, :], wdt).astype(BF16).astype(F32)
        sg = jax.nn.sigmoid(gg)
        s = gg * sg
        mid[at, :] = (s * uu).astype(BF16)
        du[at, :] = (dm * s).astype(BF16)
        dg[at, :] = (dm * uu * (sg + s * (1.0 - sg))).astype(BF16)
    dwg[...] = dot(at_[...], dg[...]).astype(BF16)
    dwu[...] = dot(at_[...], du[...]).astype(BF16)
    dwd[...] = dot(dyt[...], mid[...]).T.astype(BF16)
    run(phases, WEIGHTS_SLOTS, 2)


def weights_back(x, dy, wd, g, u, terms, chunk=256, tile=512):
    _, tokens, d = x.shape
    ff = wd.shape[0]
    whole, across, down, wide = specs(tokens, d, chunk)
    terms = blocks_of(terms)
    out = pl.pallas_call(
        functools.partial(weights_kernel, tile),
        grid=(ff // chunk,),
        out_shape=[jax.ShapeDtypeStruct((d, ff), BF16)] * 2
        + [jax.ShapeDtypeStruct((ff, d), BF16)]
        + [jax.ShapeDtypeStruct((tokens, ff), BF16)] * 2
        + [jax.ShapeDtypeStruct(t.shape[2:], BF16) for t in terms],
        in_specs=[first_of(tokens, d), whole, down, wide, wide] + [HBM] * 3,
        out_specs=[across, across, down, wide, wide] + [HBM] * 3,
        scratch_shapes=[pltpu.VMEM((d, tokens), BF16)] * 2
        + [pltpu.VMEM((tokens, chunk), BF16)]
        + reduce_scratch([t.shape for t in terms]),
        compiler_params=pltpu.CompilerParams(collective_id=2, has_side_effects=True, vmem_limit_bytes=67043328),
        name="weights_back",
    )(x, dy, wd, g, u, *terms)
    return out[:3], out[3], out[4], out[5:]


INPUT_SLOTS = (
    ((0, 0), (1, 0), (2, 0), (3, 0), (4, 0), (6, 0), (7, 0), (7, 2), (7, 2), (7, 2), (7, 2), (7, 2), (7, 2))
)


def input_kernel(tile, h, dy, wg, wu, dg, du, t0, t1, t2, dx, o0, o1, o2, da, *scratch):
    i, n = pl.program_id(0), pl.num_programs(0)
    tokens = h.shape[0]
    send, recv, local = scratch[-3:]
    phases = reducing(Place(), Sender(send, recv), (t0, t1, t2), (o0, o1, o2), scratch[:-3], local)
    run(phases, INPUT_SLOTS, 0)

    @pl.when(i == 0)
    def _():
        @by_rows(tokens)
        def _(at):
            da[at, :] = jnp.zeros((256, h.shape[1]), F32)

    wgt, wut = wg[...].T, wu[...].T
    for t in range(tokens // tile):
        at = pl.ds(t * tile, tile)
        da[at, :] += dot(dg[at, :], wgt) + dot(du[at, :], wut)

    @pl.when(i == n - 1)
    def _():
        @by_rows(tokens)
        def _(at):
            dx[at, :] = dh_rows(h, dy, da, at)

    run(phases, INPUT_SLOTS, 2)


def input_back(x, dy, wg, wu, dg, du, terms, chunk=512, tile=1024):
    _, tokens, d = x.shape
    ff = wg.shape[1]
    whole, across, down, wide = specs(tokens, d, chunk)
    terms = blocks_of(terms)
    out = pl.pallas_call(
        functools.partial(input_kernel, tile),
        grid=(ff // chunk,),
        out_shape=[jax.ShapeDtypeStruct(x.shape, BF16)] + [jax.ShapeDtypeStruct(t.shape[2:], BF16) for t in terms],
        in_specs=[first_of(tokens, d), whole, across, across, wide, wide] + [HBM] * 3,
        out_specs=[first_of(tokens, d)] + [HBM] * 3,
        scratch_shapes=[pltpu.VMEM((tokens, d), F32)] + reduce_scratch([t.shape for t in terms]),
        compiler_params=pltpu.CompilerParams(collective_id=3, has_side_effects=True, vmem_limit_bytes=67043328),
        name="input_back",
    )(x, dy, wg, wu, dg, du, *terms)
    return out[0], out[1:]


def solution(mesh):
    def step(x, dy, *weights):
        w0 = gathered(weights, 0)
        g0, u0, h1, w1 = forward(x, w0, weights, 1)
        *terms1, by_h = backward(h1, dy, w1)
        terms0, dg, du, mine1 = weights_back(x, by_h, w0[2], g0, u0, terms1)
        by_x, mine0 = input_back(x, by_h, w0[0], w0[1], dg, du, terms0)
        return (by_x, *(jnp.stack([a, b]) for a, b in zip(mine0, mine1)))

    states, cut = P(("rep", "r", "s"), None, None), P(None, "s", None)
    return jax.shard_map(
        step,
        mesh=mesh,
        in_specs=(states, states) + (cut,) * 3,
        out_specs=(states,) + (P("rep", "s", None),) * 3,
        check_vma=False,
    )
```

time: 727 us -> 410 us (0.56); the launches traced: 719 us -> 410 us
  Pallas kernels: 0 us -> 402 us
  matrix products: 395 us -> 0 us
  waiting for transfers between devices: 274 us -> 0 us
  local copies, waits for them, and re-layouts: 22.8 us -> 2.51 us
  between operations: 14.6 us -> 0.69 us
    pallas_call x0 -> x5, Pallas kernels: none -> 402 us  [the longest x1 116 us: backward(): pl.pallas_call(functools.partial(backward_kernel, tile), grid=(ff // chun...]
    dot_general x17 -> x0, matrix products: 395 us -> none  [the longest x6 142 us: layer(): up = jnp.dot(a, w['w_up'], preferred_element_type=jnp.float32)]
    reduce_scatter x6 -> x0, waiting for transfers between devices: 108 us -> none  [summed(): lax.psum_scatter(term, 's', scatter_dimension=0, tiled=True)]
    all_gather x6 -> x0, waiting for transfers between devices: 105 us -> none  [fetched(): lax.all_gather(w[number], 's', axis=0, tiled=True)]
    psum x1 -> x0, waiting for transfers between devices: 59.9 us -> none  [summed(): lax.psum(lax.psum_scatter(term, 's', scatter_dimension=0, tiled=True), 'r')]
    unnamed x37 -> x7, local copies, waits for them, and re-layouts: 16.6 us -> 2.51 us
  transfers between devices with their start and end apart: 13 -> 0, of which waited for: 10 -> 0; matrix products, arithmetic and copies ran while one was open for 44% -> 0% of each run, Pallas kernels for 0% -> 0%
where the time goes in v2:
time: 410 us
  Pallas kernels  402 us (98%)
  other arithmetic  4.7 us (1%)
    pallas_call x1, Pallas kernels, backward(): pl.pallas_call(functools.partial(backward_kernel, tile), grid=(ff // chun...  116 us
    pallas_call x1, Pallas kernels, weights_back(): pl.pallas_call(functools.partial(weights_kernel, tile), grid=(ff // chunk...  97.6 us
    pallas_call x1, Pallas kernels, input_back(): pl.pallas_call(functools.partial(input_kernel, tile), grid=(ff // chunk,)...  82.4 us
    pallas_call x1, Pallas kernels, forward(): pl.pallas_call(functools.partial(forward_kernel, tile), grid=(ff // chunk...  59.8 us
    pallas_call x1, Pallas kernels, gathered(): pl.pallas_call(gather_kernel, grid=(1,), out_shape=whole_shapes(weights),...  46.1 us

profile of v2, /device:TPU:0, one launch (start us, length us, event | category | flops | bytes accessed | tf_op | source)
XLA Modules:
  0.0 409.9 jit_solution(1480588996714653913)
XLA Ops:
  0.6 46.1 %gather_weights.1 = (bf16[4,2,80,4096]{3,2,1,0:T(8,128)(2,1)}, bf16[4,2,80,4096]{3,2,1,0:T(8,128)(2,1)}, bf16[4,2,512,640]{3,2,1,0:T(8,128)(2,1)}) custom-call(bf16[2,80,4096]{2,1,0:T(8,128)(2,1)} %ng.1, bf16[2,80,4096]{2,1,0:T(8,128)(2,1)} %nu.1, bf16[2,512,640]{2,1,0:T(8,128)(2,1)} %nd.1), custom_call_target="tpu_custom_call" | custom-call | tf_op jit(solution)/shard_map/gather_weights/pallas_call | solution.py:236
  46.7 59.8 %forward_layer.1 = (f32[2048,4096]{1,0:T(8,128)}, f32[2048,4096]{1,0:T(8,128)}, bf16[2048,640]{1,0:T(8,128)(2,1)}, bf16[4,2,80,4096]{3,2,1,0:T(8,128)(2,1)}, bf1...) custom-call(bf16[1,2048,640]{2,1,0:T(8,128)(2,1)} %h.5, bf16[640,4096]{1,0:T(8,128)(2,1)} %bitcast.20, ...), custom_call_target="tpu_custom_call" | custom-call | tf_op jit(solution)/shard_map/forward_layer/pallas_call | solution.py:606
  106.5 116.2 %backward_layer.1 = (bf16[640,4096]{1,0:T(8,128)(2,1)}, bf16[640,4096]{1,0:T(8,128)(2,1)}, bf16[4096,640]{1,0:T(8,128)(2,1)}, bf16[2048,640]{1,0:T(8,128)(2,1)}) custom-call(bf16[2048,640]{1,0:T(8,128)(2,1)} %get-tuple-element.32.h, bf16[1,2048,640]{2,1,0:T(8,128)(2,1)} %dy.1, bf16[640,4096]{1,0:T(8,128)(2,1)} %bitcast.27, bf16[640,4096]{1,0:T(8,128)(2,1)} %bitcast.28, ...), custom_call_target="tpu_custom_call" | custom-call | tf_op jit(solution)/shard_map/backward_layer/pallas_call | solution.py:665
  222.7 97.6 %weights_back.1 = (bf16[640,4096]{1,0:T(8,128)(2,1)}, bf16[640,4096]{1,0:T(8,128)(2,1)}, bf16[4096,640]{1,0:T(8,128)(2,1)}, bf16[2048,4096]{1,0:T(8,128)(2,1)}, ...) custom-call(bf16[1,2048,640]{2,1,0:T(8,128)(2,1)} %h.5, ...), custom_call_target="tpu_custom_call" | custom-call | tf_op jit(solution)/shard_map/weights_back/pallas_call | solution.py:725
  320.3 82.4 %input_back.1 = (bf16[1,2048,640]{2,1,0:T(8,128)(2,1)}, bf16[80,4096]{1,0:T(8,128)(2,1)}, bf16[80,4096]{1,0:T(8,128)(2,1)}, bf16[512,640]{1,0:T(8,128)(2,1)}) custom-call(bf16[1,2048,640]{2,1,0:T(8,128)(2,1)} %h.5, bf16[2048,640]{1,0:T(8,128)(2,1)} %get-tuple-element.36.dy, bf16[640,4096]{1,0:T(8,128)(2,1)} %bitcast.21, bf16[640,4096]{1,0:T(8,128)(2,1)} %bitcast.23, ...), custom_call_target="tpu_custom_call" | custom-call | tf_op jit(solution)/shard_map/input_back/pallas_call | solution.py:780
  402.6 0.0 copy-start.1
  402.6 0.0 copy-start.2
  402.7 3.5 pad_maximum_fusion
  406.2 0.0 copy-start
  406.2 0.0 copy-done.1
  406.2 0.0 copy-done.2
  406.2 1.2 pad_maximum_fusion.2
  407.4 1.0 copy-done
  408.4 1.5 copy.10
Async XLA Ops:
  402.6 3.5 copy-start.1
  402.6 3.5 copy-start.2
  406.2 2.2 copy-start

commit v3 on v2

--- a/solution.py
+++ b/solution.py
@@ -22,13 +22,18 @@
             return (rep, y * 4 + z, x * 2 + c)
 
         self.other = device(1 - self.c, **at)
-        self.who = {(a, k): device(self.c, **{**at, a: self.step[a][k]}) for a in "xyz" for k in (1, 2, 3)}
+        self.who = {(a, k): device(self.c, **{**at, a: self.step[a][k]}) for a in "xyz" for k in range(1, 4)}
 
     def barrier(self):
         semaphore = pltpu.get_barrier_semaphore()
-        for who in [self.other] + [self.who[a, k] for a in "xyz" for k in (1, 2, 3)]:
+        for who in [self.other] + [self.who[a, k] for a in "xyz" for k in range(1, 4)]:
             pl.semaphore_signal(semaphore, inc=1, device_id=who, device_id_type=MESH)
         pl.semaphore_wait(semaphore, 10)
+
+    def greet(self):
+        semaphore = pltpu.get_barrier_semaphore()
+        pl.semaphore_signal(semaphore, inc=1, device_id=self.other, device_id_type=MESH)
+        pl.semaphore_wait(semaphore, 1)
 
 
 class Copy:
@@ -74,8 +79,69 @@
             made.wait_send()
 
 
-def run(phases, slots, position):
-    for phase, (step, place) in zip(phases, slots, strict=True):
+class Swap:
+    def __init__(self, me, held, outs, send, recv, chunk):
+        self.me, self.held, self.outs, self.send, self.recv, self.chunk = me, held, outs, send, recv, chunk
+        self.rows = outs[2].shape[1]
+
+    def theirs(self, i):
+        return (i * self.chunk // self.rows) % 2 != self.me.c
+
+    def copy(self, k, i):
+        first = i * self.chunk
+        if k < 2:
+            dst = self.outs[k].at[:, :, pl.ds(pl.multiple_of(first, self.chunk), self.chunk)]
+        else:
+            dst = self.outs[2].at[first // self.rows // 2, pl.ds(pl.multiple_of(first % self.rows, self.chunk), self.chunk)]
+        return pltpu.make_async_remote_copy(
+            src_ref=self.held[k],
+            dst_ref=dst,
+            send_sem=self.send.at[k],
+            recv_sem=self.recv.at[k, i],
+            device_id=self.me.other,
+            device_id_type=MESH,
+        )
+
+    def sent(self, i):
+        for k in (0, 1):
+            self.copy(k, i).wait_send()
+        pl.when(self.theirs(i))(lambda: self.copy(2, i).wait_send())
+
+    def step(self, i, n, *made):
+        pl.when(i > 0)(lambda: self.sent(i - 1))
+        block = made[0].shape[0] // 8
+        for k in (0, 1):
+            for x in range(4):
+                at = pl.multiple_of((2 * x + 1 - self.me.c) * block, 16)
+                self.held[k][x] = made[k][pl.ds(at, block), :]
+            self.copy(k, i).start()
+
+        @pl.when(self.theirs(i))
+        def _():
+            self.held[2][...] = made[2][...]
+            self.copy(2, i).start()
+
+        @pl.when(i == n - 1)
+        def _():
+            self.sent(i)
+            for j in range(n):
+                for k in (0, 1):
+                    self.copy(k, j).wait_recv()
+                pl.when(jnp.logical_not(self.theirs(j)))(lambda: self.copy(2, j).wait_recv())
+
+
+def swap_scratch(d, ff, chunk):
+    held = [pltpu.VMEM((4, d // 8, chunk), BF16)] * 2 + [pltpu.VMEM((chunk, d), BF16)]
+    return held + [pltpu.SemaphoreType.DMA((3,)), pltpu.SemaphoreType.DMA((3, ff // chunk))]
+
+
+def swap_shapes(d, ff):
+    return [jax.ShapeDtypeStruct((4, d // 8, ff), BF16)] * 2 + [jax.ShapeDtypeStruct((4, ff // 8, d), BF16)]
+
+
+def run(phases, slots, position, steps):
+    for phase, slot in zip(phases, slots, strict=True):
+        step, place = (steps - 1, 2) if slot == 2 * steps else divmod(slot, 2)
         if place == position:
             pl.when(pl.program_id(0) == step)(phase)
 
@@ -101,7 +167,7 @@
         return self.out.at[x, c, :, d] if self.dim else self.out.at[x, c, d]
 
 
-GATHER_COPIES = 3 + 4 * 31
+GATHER_COPIES = 3 + 4 * 28
 
 
 def gathering(me, go, owns, outs, local):
@@ -140,9 +206,9 @@
                 second=[on(p, x3, q, 0, who["x", 1]), on(p, x1, q, 1, who["x", 3])],
                 along=[[on(p, at, q, None, to) for to in (up, down)] for at in (x3, x1, x2)],
                 across=[on(p, at, q, None, other) for at in (x3, x1, x2)],
+                passed=[[on(p, at, k, None, other) for k in (q3, q1)] for at in (x3, x1, x2)],
+                whole=[on(p, at, q2, None, other) for at in (x3, x1, x2)],
                 last=[[on(p, at, q3, 0, up), on(p, at, q1, 1, down)] for at in (x3, x1, x2)],
-                across1=[[on(p, at, q3, None, other), on(p, at, q1, None, other)] for at in (x3, x1, x2)],
-                across2=[[on(p, at, q2, half, other) for half in (0, 1)] for at in (x3, x1, x2)],
             )
         )
 
@@ -161,17 +227,15 @@
             for k in (0, 1):
                 t["first"][k].wait_recv()
                 t["second"][k].start()
-                for i in t["along"][k]:
+                for i in [*t["along"][k], t["across"][k]]:
                     i.start()
-                t["across"][k].start()
 
     def far():
         for t in plans:
             for i in t["second"]:
                 i.wait_recv()
-            for i in t["along"][2]:
+            for i in [*t["along"][2], t["across"][2]]:
                 i.start()
-            t["across"][2].start()
 
     def turn(k):
         def phase():
@@ -179,31 +243,28 @@
                 for j in (0, 1):
                     t["along"][k][j].wait_recv()
                     t["last"][k][j].start()
-                    t["across1"][k][j].start()
+                    t["passed"][k][j].start()
 
         return phase
 
-    def ends(ks):
-        def phase():
-            for k in ks:
-                for t in plans:
-                    for j in (0, 1):
-                        t["last"][k][j].wait_recv()
-                        t["across2"][k][j].start()
-
-        return phase
+    def ends():
+        for k in range(3):
+            for t in plans:
+                for i in t["last"][k]:
+                    i.wait_recv()
+                t["whole"][k].start()
 
     def finish():
         for i in swaps:
             i.wait_recv()
         for t in plans:
-            for i in t["across"] + sum(t["across1"] + t["across2"], []):
+            for i in t["across"] + sum(t["passed"], t["whole"]):
                 i.wait_recv()
         for i in here:
             i.wait()
         go.finish()
 
-    return [start, hand_on, far, turn(0), turn(1), turn(2), ends((0, 1, 2)), finish]
+    return [start, hand_on, far, turn(0), turn(1), turn(2), ends, finish]
 
 
 GATHER_SCRATCH = [
@@ -253,17 +314,23 @@
             added(dst.at[i], *(s.at[i] for s in srcs))
         return
     rows, columns = shape
-    step = 16 if rows % 16 == 0 else rows
-    wide = min(columns, 1024)
-
-    @pl.loop(0, rows // step)
-    def _(i):
-        for j in range(0, columns, wide):
-            at = (pl.ds(pl.multiple_of(i * step, step), step), pl.ds(j, min(wide, columns - j)))
-            total = srcs[0][at].astype(F32)
-            for s in srcs[1:]:
-                total = total + s[at].astype(F32)
-            dst[at] = total.astype(dst.dtype)
+    wide = 512 if columns > 1024 else columns
+    tall = rows
+    while tall * wide > 49152 and tall % 32 == 0:
+        tall //= 2
+
+    def block(i, j):
+        at = (pl.ds(pl.multiple_of(i, 16), tall), pl.ds(pl.multiple_of(j, 128), wide))
+        total = srcs[0][at].astype(F32)
+        for s in srcs[1:]:
+            total = total + s[at].astype(F32)
+        dst[at] = total.astype(dst.dtype)
+
+    if wide < columns:
+        pl.loop(0, columns // wide)(lambda j: block(0, j * wide))
+    else:
+        for i in range(rows // tall):
+            block(i * tall, 0)
 
 
 class Ring:
@@ -278,14 +345,8 @@
 
             return src, piece, half, go.copy(lambda: (src(), got.at[k]), to)
 
-        self.slots = [
-            slot(0, 2, 0, up),
-            slot(1, 2, 1, down),
-            slot(2, 1, 1, up),
-            slot(3, 3, 0, down),
-            slot(4, 1, 0, up),
-            slot(5, 3, 1, down),
-        ]
+        order = ((2, 0), (2, 1), (1, 1), (3, 0), (1, 0), (3, 1))
+        self.slots = [slot(k, *which, down if k % 2 else up) for k, which in enumerate(order)]
 
     def term(self, piece, half):
         return [self.cut(t, self.at[piece], half) for t in self.terms]
@@ -305,22 +366,42 @@
             self.send(4 + k, self.got.at[k])
 
     def end(self, cut_out):
-        for k in (2, 3, 4, 5):
+        for k in range(2, 6):
             self.slots[k][3].wait_recv()
         added(cut_out(self.out, 0), *self.term(0, 0), self.got.at[3], self.got.at[4])
         added(cut_out(self.out, 1), *self.term(0, 1), self.got.at[2], self.got.at[5])
+
+
+class Direct:
+    def __init__(self, me, go, axis, terms, cut, out, got, hold):
+        self.term, self.cut, self.out, self.got, self.hold, self.at = terms[0], cut, out, got, hold, me.step[axis]
+        self.sent = [self.copy(go, k, me.who[axis, k + 1]) for k in range(3)]
+
+    def copy(self, go, k, to):
+        return go.copy(lambda: (self.hold.at[k], self.got.at[k]), to)
+
+    def start(self):
+        for k, copy in enumerate(self.sent):
+            added(self.hold.at[k], self.cut(self.term, self.at[k + 1], None))
+            copy.start()
+
+    def end(self, _):
+        for copy in self.sent:
+            copy.wait_recv()
+        added(self.out, self.cut(self.term, self.at[0], None), *(self.got.at[k] for k in range(3)))
 
 
 def piece(dim, n):
     def cut(ref, q, half):
         w = ref.shape[dim] // 4
         at = [slice(None)] * len(ref.shape)
-        if n == dim:
+        if n == dim and half is not None:
             at[dim] = pl.ds(pl.multiple_of(q * w + half * (w // 2), w // 2), w // 2)
         else:
             at[dim] = pl.ds(pl.multiple_of(q * w, w), w)
-            h = ref.shape[n] // 2
-            at[n] = pl.ds(half * h, h)
+            if half is not None:
+                h = ref.shape[n] // 2
+                at[n] = pl.ds(half * h, h)
         if dim == 0 and len(ref.shape) == 3:
             at[0] = q
         return ref.at[tuple(at)]
@@ -362,10 +443,10 @@
     return sizes
 
 
-REDUCE_COPIES = 3 * (1 + 18 + 3 + 4)
-
-
-def reducing(me, go, terms, outs, scratch, local):
+REDUCE_COPIES = 3 * (12 + 3 + 3 + 4)
+
+
+def reducing(me, go, terms, arrived, outs, scratch, local):
     c = me.c
     per = len(scratch) // 3
     bufs = [scratch[m * per : (m + 1) * per] for m in range(3)]
@@ -374,7 +455,7 @@
         return Copy(lambda: pltpu.make_async_copy(terms[m].at[:, c], bufs[m][0], local.at[m]))
 
     def swap(m):
-        return go.copy(lambda: (terms[m].at[:, 1 - c], bufs[m][1]), me.other)
+        return Copy(lambda: pltpu.make_async_copy(arrived[m], bufs[m][1], local.at[6 + m]))
 
     here, swaps = [own(m) for m in range(3)], [swap(m) for m in range(3)]
     rings = []
@@ -384,7 +465,8 @@
         for k, (axis, dim, n) in enumerate(steps):
             t = (b[0], b[1]) if k == 0 else (made[-1].out,)
             at = 2 if k == 0 else 4 + 3 * (k - 1)
-            made.append(Ring(me, go, axis, t, piece(dim, n), b[at], b[at + 1], None if k == 0 else b[at + 2]))
+            kind = Ring if k < 2 else Direct
+            made.append(kind(me, go, axis, t, piece(dim, n), b[at], b[at + 1], b[at + 2] if k else None))
             made[-1].halves = halves(n - 1 if dim == 0 and len(t[0].shape) == 3 else n)
         rings.append(made)
 
@@ -411,7 +493,7 @@
         spread.append(
             dict(
                 mine=lambda at=at, h=h, l=l: at(h, l),
-                low=[copy(me.who[low, k], h, l) for k in (1, 2, 3)],
+                low=[copy(me.who[low, k], h, l) for k in range(1, 4)],
                 near=[copy(me.who[high, 1], h), copy(me.who[high, 3], h)],
                 far=[copy(me.who[high, 1], h3, None, 0), copy(me.who[high, 3], h1, None, 1)],
             )
@@ -421,16 +503,15 @@
     ]
 
     def start():
-        for i in here:
-            i.start()
+        for m in range(3):
+            here[m].start()
+            swaps[m].start()
         me.barrier()
-        for i in swaps:
-            i.start()
 
     def first(m):
         def phase():
             here[m].wait()
-            swaps[m].wait_recv()
+            swaps[m].wait()
             rings[m][0].start()
 
         return phase
@@ -480,7 +561,7 @@
             i.wait()
         go.finish()
 
-    return [start, first(0), first(1), first(2), middle(0), end(0), middle(1), end(1), middle(2), low, near, far, finish]
+    return [start, first(0), first(1), first(2), middle(0), end(0), middle(1), end(1), low, near, far, finish]
 
 
 def reduce_scratch(shapes):
@@ -489,39 +570,18 @@
         block = (4, *s[2:])
         scratch += [pltpu.VMEM(block, BF16)] * 2
         for k, (half, whole) in enumerate(plan(block, ROUTES[m][1])):
-            scratch += [pltpu.VMEM(whole, F32), pltpu.VMEM((6, *half), BF16)]
-            if k:
-                scratch.append(pltpu.VMEM((6, *half), BF16))
+            many = (6, *half) if k < 2 else (3, *whole)
+            scratch += [pltpu.VMEM(whole, F32)] + [pltpu.VMEM(many, BF16)] * (2 if k else 1)
         scratch.append(pltpu.VMEM(s[2:], BF16))
     return scratch + [
         pltpu.SemaphoreType.DMA((REDUCE_COPIES,)),
         pltpu.SemaphoreType.DMA((REDUCE_COPIES,)),
-        pltpu.SemaphoreType.DMA((6,)),
+        pltpu.SemaphoreType.DMA((9,)),
     ]
 
 
 def blocks_of(terms):
     return [t.reshape(4, 2, t.shape[0] // 8, t.shape[1]) for t in terms]
-
-
-def reduce_kernel(*refs):
-    terms, outs, scratch = refs[:3], refs[3:6], refs[6:]
-    send, recv, local = scratch[-3:]
-    for phase in reducing(Place(), Sender(send, recv), terms, outs, scratch[:-3], local):
-        phase()
-
-
-def reduced(terms):
-    terms = blocks_of(terms)
-    return pl.pallas_call(
-        reduce_kernel,
-        out_shape=[jax.ShapeDtypeStruct(t.shape[2:], BF16) for t in terms],
-        in_specs=[HBM] * 3,
-        out_specs=[HBM] * 3,
-        scratch_shapes=reduce_scratch([t.shape for t in terms]),
-        compiler_params=pltpu.CompilerParams(collective_id=1, has_side_effects=True, vmem_limit_bytes=60 * 2**20),
-        name="reduce_gradients",
-    )(*terms)
 
 
 def dot(a, b):
@@ -550,14 +610,14 @@
     return dy[at, :] + by_h
 
 
-FORWARD_SLOTS = ((0, 0), (2, 0), (3, 0), (3, 1), (4, 1), (5, 1), (6, 1), (7, 2))
-
-
-def forward_kernel(tile, h, wg, wu, wd, ng, nu, nd, g_out, u_out, h_out, og, ou, od, a, acc, send, recv, local):
+FORWARD_SLOTS = (0, 4, 6, 7, 9, 11, 13, 16)
+
+
+def forward_kernel(tile, steps, h, wg, wu, wd, ng, nu, nd, g_out, u_out, h_out, og, ou, od, a, acc, send, recv, local):
     i, n = pl.program_id(0), pl.num_programs(0)
     tokens = h.shape[0]
     phases = gathering(Place(), Sender(send, recv), [w.at[0] for w in (ng, nu, nd)], (og, ou, od), local)
-    run(phases, FORWARD_SLOTS, 0)
+    run(phases, FORWARD_SLOTS, 0, steps)
 
     @pl.when(i == 0)
     def _():
@@ -569,7 +629,7 @@
 
     for t in range(tokens // tile):
         if t:
-            run(phases, FORWARD_SLOTS, t)
+            run(phases, FORWARD_SLOTS, t, steps)
         at = pl.ds(t * tile, tile)
         g = dot(a[at, :], wg[...])
         u = dot(a[at, :], wu[...])
@@ -584,7 +644,7 @@
         def _(at):
             h_out[at, :] = h[at, :] + acc[at, :].astype(BF16)
 
-    run(phases, FORWARD_SLOTS, 2)
+    run(phases, FORWARD_SLOTS, 2, steps)
 
 
 def specs(tokens, d, chunk):
@@ -604,7 +664,7 @@
     ff = w[0].shape[1]
     whole, across, down, wide = specs(tokens, d, chunk)
     out = pl.pallas_call(
-        functools.partial(forward_kernel, tile),
+        functools.partial(forward_kernel, tile, ff // chunk),
         grid=(ff // chunk,),
         out_shape=[jax.ShapeDtypeStruct((tokens, ff), F32)] * 2
         + [jax.ShapeDtypeStruct((tokens, d), BF16)]
@@ -618,9 +678,14 @@
     return out[0], out[1], out[2], flat(out[3:])
 
 
-def backward_kernel(tile, h, dy, wg, wu, wd, dwg, dwu, dwd, dh, a, at_, dyt, da, mid, dg, du):
+def backward_kernel(
+    tile, steps, h, dy, wg, wu, wd, dwg, dwu, dwd, dh, r0, r1, r2, a, at_, dyt, da, mid, dg, du, h0, h1, h2, send, recv
+):
     i, n = pl.program_id(0), pl.num_programs(0)
-    tokens = h.shape[0]
+    tokens, chunk = h.shape[0], wg.shape[1]
+    me = Place()
+    swap = Swap(me, (h0, h1, h2), (r0, r1, r2), send, recv, chunk)
+    pl.when(i == 0)(me.greet)
 
     @pl.when(i == 0)
     def _():
@@ -657,41 +722,51 @@
         def _(at):
             dh[at, :] = dh_rows(h, dy, da, at)
 
+    swap.step(i, steps, dwg, dwu, dwd)
+
 
 def backward(h, dy, w, chunk=512, tile=1024):
     tokens, d = h.shape
     ff = w[0].shape[1]
     whole, across, down, wide = specs(tokens, d, chunk)
-    return pl.pallas_call(
-        functools.partial(backward_kernel, tile),
+    out = pl.pallas_call(
+        functools.partial(backward_kernel, tile, ff // chunk),
         grid=(ff // chunk,),
         out_shape=[jax.ShapeDtypeStruct((d, ff), BF16)] * 2
-        + [jax.ShapeDtypeStruct((ff, d), BF16), jax.ShapeDtypeStruct((tokens, d), BF16)],
+        + [jax.ShapeDtypeStruct((ff, d), BF16), jax.ShapeDtypeStruct((tokens, d), BF16)]
+        + swap_shapes(d, ff),
         in_specs=[whole, first_of(tokens, d), across, across, down],
-        out_specs=[across, across, down, whole],
+        out_specs=[across, across, down, whole] + [HBM] * 3,
         scratch_shapes=[
             pltpu.VMEM((tokens, d), BF16),
             pltpu.VMEM((d, tokens), BF16),
             pltpu.VMEM((d, tokens), BF16),
             pltpu.VMEM((tokens, d), F32),
         ]
-        + [pltpu.VMEM((tokens, chunk), BF16)] * 3,
-        compiler_params=pltpu.CompilerParams(vmem_limit_bytes=62 * 2**20),
+        + [pltpu.VMEM((tokens, chunk), BF16)] * 3
+        + swap_scratch(d, ff, chunk),
+        compiler_params=pltpu.CompilerParams(collective_id=4, has_side_effects=True, vmem_limit_bytes=67043328),
         name="backward_layer",
     )(h, dy, *w)
-
-
-WEIGHTS_SLOTS = (
-    ((0, 0), (2, 0), (3, 0), (4, 0), (5, 0), (7, 0), (8, 0), (9, 0), (10, 0), (11, 0), (12, 0), (13, 0), (15, 2))
-)
-
-
-def weights_kernel(tile, h, dy, wd, g, u, t0, t1, t2, dwg, dwu, dwd, dg, du, o0, o1, o2, at_, dyt, mid, *scratch):
+    return out[:3], out[3], out[4:]
+
+
+WEIGHTS_SLOTS = (0, *(2,) * 3, 8, 14, 16, 20, 24, 26, 30, 32)
+
+
+def weights_kernel(tile, steps, h, dy, wd, g, u, *refs):
+    refs = iter(refs)
+    terms, arrived, (dwg, dwu, dwd), (dg, du), outs, swapped, (at_, dyt, mid), held, (to, come) = (
+        [next(refs) for _ in name] for name in ("tgu", "rgu", "gud", "gu", "ogu", "sgu", "adm", "hgu", "tc")
+    )
+    scratch = list(refs)
     i = pl.program_id(0)
-    tokens = h.shape[0]
+    tokens, chunk = h.shape[0], wd.shape[0]
     send, recv, local = scratch[-3:]
-    phases = reducing(Place(), Sender(send, recv), (t0, t1, t2), (o0, o1, o2), scratch[:-3], local)
-    run(phases, WEIGHTS_SLOTS, 0)
+    me = Place()
+    swap = Swap(me, held, swapped, to, come, chunk)
+    phases = reducing(me, Sender(send, recv), terms, arrived, outs, scratch[:-3], local)
+    run(phases, WEIGHTS_SLOTS, 0, steps)
 
     @pl.when(i == 0)
     def _():
@@ -714,43 +789,44 @@
     dwg[...] = dot(at_[...], dg[...]).astype(BF16)
     dwu[...] = dot(at_[...], du[...]).astype(BF16)
     dwd[...] = dot(dyt[...], mid[...]).T.astype(BF16)
-    run(phases, WEIGHTS_SLOTS, 2)
-
-
-def weights_back(x, dy, wd, g, u, terms, chunk=256, tile=512):
+    swap.step(i, steps, dwg, dwu, dwd)
+    run(phases, WEIGHTS_SLOTS, 2, steps)
+
+
+def weights_back(x, dy, wd, g, u, terms, arrived, chunk=256, tile=512):
     _, tokens, d = x.shape
     ff = wd.shape[0]
     whole, across, down, wide = specs(tokens, d, chunk)
     terms = blocks_of(terms)
     out = pl.pallas_call(
-        functools.partial(weights_kernel, tile),
+        functools.partial(weights_kernel, tile, ff // chunk),
         grid=(ff // chunk,),
         out_shape=[jax.ShapeDtypeStruct((d, ff), BF16)] * 2
         + [jax.ShapeDtypeStruct((ff, d), BF16)]
         + [jax.ShapeDtypeStruct((tokens, ff), BF16)] * 2
-        + [jax.ShapeDtypeStruct(t.shape[2:], BF16) for t in terms],
-        in_specs=[first_of(tokens, d), whole, down, wide, wide] + [HBM] * 3,
-        out_specs=[across, across, down, wide, wide] + [HBM] * 3,
+        + [jax.ShapeDtypeStruct(t.shape[2:], BF16) for t in terms]
+        + swap_shapes(d, ff),
+        in_specs=[first_of(tokens, d), whole, down, wide, wide] + [HBM] * 6,
+        out_specs=[across, across, down, wide, wide] + [HBM] * 6,
         scratch_shapes=[pltpu.VMEM((d, tokens), BF16)] * 2
         + [pltpu.VMEM((tokens, chunk), BF16)]
+        + swap_scratch(d, ff, chunk)
         + reduce_scratch([t.shape for t in terms]),
         compiler_params=pltpu.CompilerParams(collective_id=2, has_side_effects=True, vmem_limit_bytes=67043328),
         name="weights_back",
-    )(x, dy, wd, g, u, *terms)
-    return out[:3], out[3], out[4], out[5:]
-
-
-INPUT_SLOTS = (
-    ((0, 0), (1, 0), (2, 0), (3, 0), (4, 0), (6, 0), (7, 0), (7, 2), (7, 2), (7, 2), (7, 2), (7, 2), (7, 2))
-)
-
-
-def input_kernel(tile, h, dy, wg, wu, dg, du, t0, t1, t2, dx, o0, o1, o2, da, *scratch):
+    )(x, dy, wd, g, u, *terms, *arrived)
+    return out[:3], out[3], out[4], out[5:8], out[8:]
+
+
+INPUT_SLOTS = (0, *(2,) * 3, 6, 10, 12, 14, *(16,) * 4)
+
+
+def input_kernel(tile, steps, h, dy, wg, wu, dg, du, t0, t1, t2, r0, r1, r2, dx, o0, o1, o2, da, *scratch):
     i, n = pl.program_id(0), pl.num_programs(0)
     tokens = h.shape[0]
     send, recv, local = scratch[-3:]
-    phases = reducing(Place(), Sender(send, recv), (t0, t1, t2), (o0, o1, o2), scratch[:-3], local)
-    run(phases, INPUT_SLOTS, 0)
+    phases = reducing(Place(), Sender(send, recv), (t0, t1, t2), (r0, r1, r2), (o0, o1, o2), scratch[:-3], local)
+    run(phases, INPUT_SLOTS, 0, steps)
 
     @pl.when(i == 0)
     def _():
@@ -760,6 +836,8 @@
 
     wgt, wut = wg[...].T, wu[...].T
     for t in range(tokens // tile):
+        if t:
+            run(phases, INPUT_SLOTS, t, steps)
         at = pl.ds(t * tile, tile)
         da[at, :] += dot(dg[at, :], wgt) + dot(du[at, :], wut)
 
@@ -769,24 +847,24 @@
         def _(at):
             dx[at, :] = dh_rows(h, dy, da, at)
 
-    run(phases, INPUT_SLOTS, 2)
-
-
-def input_back(x, dy, wg, wu, dg, du, terms, chunk=512, tile=1024):
+    run(phases, INPUT_SLOTS, 2, steps)
+
+
+def input_back(x, dy, wg, wu, dg, du, terms, arrived, chunk=512, tile=1024):
     _, tokens, d = x.shape
     ff = wg.shape[1]
     whole, across, down, wide = specs(tokens, d, chunk)
     terms = blocks_of(terms)
     out = pl.pallas_call(
-        functools.partial(input_kernel, tile),
+        functools.partial(input_kernel, tile, ff // chunk),
         grid=(ff // chunk,),
         out_shape=[jax.ShapeDtypeStruct(x.shape, BF16)] + [jax.ShapeDtypeStruct(t.shape[2:], BF16) for t in terms],
-        in_specs=[first_of(tokens, d), whole, across, across, wide, wide] + [HBM] * 3,
+        in_specs=[first_of(tokens, d), whole, across, across, wide, wide] + [HBM] * 6,
         out_specs=[first_of(tokens, d)] + [HBM] * 3,
         scratch_shapes=[pltpu.VMEM((tokens, d), F32)] + reduce_scratch([t.shape for t in terms]),
         compiler_params=pltpu.CompilerParams(collective_id=3, has_side_effects=True, vmem_limit_bytes=67043328),
         name="input_back",
-    )(x, dy, wg, wu, dg, du, *terms)
+    )(x, dy, wg, wu, dg, du, *terms, *arrived)
     return out[0], out[1:]
 
 
@@ -794,9 +872,9 @@
     def step(x, dy, *weights):
         w0 = gathered(weights, 0)
         g0, u0, h1, w1 = forward(x, w0, weights, 1)
-        *terms1, by_h = backward(h1, dy, w1)
-        terms0, dg, du, mine1 = weights_back(x, by_h, w0[2], g0, u0, terms1)
-        by_x, mine0 = input_back(x, by_h, w0[0], w0[1], dg, du, terms0)
+        terms1, by_h, arrived1 = backward(h1, dy, w1)
+        terms0, dg, du, mine1, arrived0 = weights_back(x, by_h, w0[2], g0, u0, terms1, arrived1)
+        by_x, mine0 = input_back(x, by_h, w0[0], w0[1], dg, du, terms0, arrived0)
         return (by_x, *(jnp.stack([a, b]) for a, b in zip(mine0, mine1)))
 
     states, cut = P(("rep", "r", "s"), None, None), P(None, "s", None)

time: 410 us -> 388 us (0.946)
  Pallas kernels: 402 us -> 380 us
    pallas_call x4, Pallas kernels: 356 us -> 334 us  [the longest x1 120 us: backward(): pl.pallas_call(functools.partial(backward_kernel, tile, ff // chunk), gri...]
where the time goes in v3:
time: 388 us
  Pallas kernels  380 us (98%)
  other arithmetic  4.7 us (1%)
    pallas_call x1, Pallas kernels, backward(): pl.pallas_call(functools.partial(backward_kernel, tile, ff // chunk), gri...  120 us
    pallas_call x1, Pallas kernels, weights_back(): pl.pallas_call(functools.partial(weights_kernel, tile, ff // chunk), grid...  84.4 us
    pallas_call x1, Pallas kernels, input_back(): pl.pallas_call(functools.partial(input_kernel, tile, ff // chunk), grid=(...  70.4 us
    pallas_call x1, Pallas kernels, forward(): pl.pallas_call(functools.partial(forward_kernel, tile, ff // chunk), grid...  59.4 us
    pallas_call x1, Pallas kernels, gathered(): pl.pallas_call(gather_kernel, grid=(1,), out_shape=whole_shapes(weights),...  45.9 us

profile of v3, /device:TPU:0, one launch (start us, length us, event | category | flops | bytes accessed | tf_op | source)
XLA Modules:
  0.0 388.2 jit_solution(7578725883915081556)
XLA Ops:
  0.6 45.9 %gather_weights.1 = (bf16[4,2,80,4096]{3,2,1,0:T(8,128)(2,1)}, bf16[4,2,80,4096]{3,2,1,0:T(8,128)(2,1)}, bf16[4,2,512,640]{3,2,1,0:T(8,128)(2,1)}) custom-call(bf16[2,80,4096]{2,1,0:T(8,128)(2,1)} %ng.1, bf16[2,80,4096]{2,1,0:T(8,128)(2,1)} %nu.1, bf16[2,512,640]{2,1,0:T(8,128)(2,1)} %nd.1), custom_call_target="tpu_custom_call" | custom-call | tf_op jit(solution)/shard_map/gather_weights/pallas_call | solution.py:297
  46.5 59.4 %forward_layer.1 = (f32[2048,4096]{1,0:T(8,128)}, f32[2048,4096]{1,0:T(8,128)}, bf16[2048,640]{1,0:T(8,128)(2,1)}, bf16[4,2,80,4096]{3,2,1,0:T(8,128)(2,1)}, bf1...) custom-call(bf16[1,2048,640]{2,1,0:T(8,128)(2,1)} %h.5, bf16[640,4096]{1,0:T(8,128)(2,1)} %bitcast.18, ...), custom_call_target="tpu_custom_call" | custom-call | tf_op jit(solution)/shard_map/forward_layer/pallas_call | solution.py:666
  105.9 120.2 %backward_layer.1 = (bf16[640,4096]{1,0:T(8,128)(2,1)}, bf16[640,4096]{1,0:T(8,128)(2,1)}, bf16[4096,640]{1,0:T(8,128)(2,1)}, bf16[2048,640]{1,0:T(8,128)(2,1)},...) custom-call(bf16[2048,640]{1,0:T(8,128)(2,1)} %get-tuple-element.38.h, ...), custom_call_target="tpu_custom_call" | custom-call | tf_op jit(solution)/shard_map/backward_layer/pallas_call | solution.py:732
  226.1 84.4 %weights_back.1 = (bf16[640,4096]{1,0:T(8,128)(2,1)}, bf16[640,4096]{1,0:T(8,128)(2,1)}, bf16[4096,640]{1,0:T(8,128)(2,1)}, bf16[2048,4096]{1,0:T(8,128)(2,1)}, ...) custom-call(bf16[1,2048,640]{2,1,0:T(8,128)(2,1)} %h.5, ...), custom_call_target="tpu_custom_call" | custom-call | tf_op jit(solution)/shard_map/weights_back/pallas_call | solution.py:801
  310.5 70.4 %input_back.1 = (bf16[1,2048,640]{2,1,0:T(8,128)(2,1)}, bf16[80,4096]{1,0:T(8,128)(2,1)}, bf16[80,4096]{1,0:T(8,128)(2,1)}, bf16[512,640]{1,0:T(8,128)(2,1)}) custom-call(bf16[1,2048,640]{2,1,0:T(8,128)(2,1)} %h.5, bf16[2048,640]{1,0:T(8,128)(2,1)} %get-tuple-element.42.dy, bf16[640,4096]{1,0:T(8,128)(2,1)} %bitcast.19, bf16[640,4096]{1,0:T(8,128)(2,1)} %bitcast.21, ...), custom_call_target="tpu_custom_call" | custom-call | tf_op jit(solution)/shard_map/input_back/pallas_call | solution.py:858
  381.0 0.0 copy-start.1
  381.0 0.0 copy-start.2
  381.0 3.5 pad_maximum_fusion
  384.5 0.0 copy-start
  384.5 0.0 copy-done.1
  384.5 0.0 copy-done.2
  384.5 1.2 pad_maximum_fusion.2
  385.7 1.0 copy-done
  386.7 1.5 copy.10
Async XLA Ops:
  381.0 3.5 copy-start.1
  381.0 3.5 copy-start.2
  384.5 2.2 copy-start

commit v4 on v3

--- a/solution.py
+++ b/solution.py
@@ -698,7 +698,7 @@
             dyt[:, at] = dy[at, :].T
             da[at, :] = jnp.zeros((256, h.shape[1]), F32)
 
-    wdt, wgt, wut = wd[...].T, wg[...].T, wu[...].T
+    wdt, wgut = wd[...].T, jnp.concatenate([wg[...], wu[...]], 1).T
     for t in range(tokens // tile):
         at = pl.ds(t * tile, tile)
         g = dot(a[at, :], wg[...])
@@ -711,7 +711,7 @@
         dgb = (dm * u * (sg + s * (1.0 - sg))).astype(BF16)
         du[at, :] = dub
         dg[at, :] = dgb
-        da[at, :] += dot(dgb, wgt) + dot(dub, wut)
+        da[at, :] += dot(jnp.concatenate([dgb, dub], 1), wgut)
     dwg[...] = dot(at_[...], dg[...]).astype(BF16)
     dwu[...] = dot(at_[...], du[...]).astype(BF16)
     dwd[...] = dot(dyt[...], mid[...]).T.astype(BF16)
@@ -834,12 +834,12 @@
         def _(at):
             da[at, :] = jnp.zeros((256, h.shape[1]), F32)
 
-    wgt, wut = wg[...].T, wu[...].T
+    wgut = jnp.concatenate([wg[...], wu[...]], 1).T
     for t in range(tokens // tile):
         if t:
             run(phases, INPUT_SLOTS, t, steps)
         at = pl.ds(t * tile, tile)
-        da[at, :] += dot(dg[at, :], wgt) + dot(du[at, :], wut)
+        da[at, :] += dot(jnp.concatenate([dg[at, :], du[at, :]], 1), wgut)
 
     @pl.when(i == n - 1)
     def _():

time: 388 us -> 387 us (level)
  no operation moved by 1% of the time
where the time goes in v4:
time: 387 us
  Pallas kernels  379 us (98%)
  other arithmetic  4.7 us (1%)
    pallas_call x1, Pallas kernels, backward(): pl.pallas_call(functools.partial(backward_kernel, tile, ff // chunk), gri...  119 us
    pallas_call x1, Pallas kernels, weights_back(): pl.pallas_call(functools.partial(weights_kernel, tile, ff // chunk), grid...  84.4 us
    pallas_call x1, Pallas kernels, input_back(): pl.pallas_call(functools.partial(input_kernel, tile, ff // chunk), grid=(...  70.4 us
    pallas_call x1, Pallas kernels, forward(): pl.pallas_call(functools.partial(forward_kernel, tile, ff // chunk), grid...  59.4 us
    pallas_call x1, Pallas kernels, gathered(): pl.pallas_call(gather_kernel, grid=(1,), out_shape=whole_shapes(weights),...  45.9 us

profile of v4, /device:TPU:0, one launch (start us, length us, event | category | flops | bytes accessed | tf_op | source)
XLA Modules:
  0.0 387.3 jit_solution(6949053600027919279)
XLA Ops:
  0.6 45.9 %gather_weights.1 = (bf16[4,2,80,4096]{3,2,1,0:T(8,128)(2,1)}, bf16[4,2,80,4096]{3,2,1,0:T(8,128)(2,1)}, bf16[4,2,512,640]{3,2,1,0:T(8,128)(2,1)}) custom-call(bf16[2,80,4096]{2,1,0:T(8,128)(2,1)} %ng.1, bf16[2,80,4096]{2,1,0:T(8,128)(2,1)} %nu.1, bf16[2,512,640]{2,1,0:T(8,128)(2,1)} %nd.1), custom_call_target="tpu_custom_call" | custom-call | tf_op jit(solution)/shard_map/gather_weights/pallas_call | solution.py:297
  46.5 59.4 %forward_layer.1 = (f32[2048,4096]{1,0:T(8,128)}, f32[2048,4096]{1,0:T(8,128)}, bf16[2048,640]{1,0:T(8,128)(2,1)}, bf16[4,2,80,4096]{3,2,1,0:T(8,128)(2,1)}, bf1...) custom-call(bf16[1,2048,640]{2,1,0:T(8,128)(2,1)} %h.5, bf16[640,4096]{1,0:T(8,128)(2,1)} %bitcast.18, ...), custom_call_target="tpu_custom_call" | custom-call | tf_op jit(solution)/shard_map/forward_layer/pallas_call | solution.py:666
  105.9 119.2 %backward_layer.1 = (bf16[640,4096]{1,0:T(8,128)(2,1)}, bf16[640,4096]{1,0:T(8,128)(2,1)}, bf16[4096,640]{1,0:T(8,128)(2,1)}, bf16[2048,640]{1,0:T(8,128)(2,1)},...) custom-call(bf16[2048,640]{1,0:T(8,128)(2,1)} %get-tuple-element.38.h, ...), custom_call_target="tpu_custom_call" | custom-call | tf_op jit(solution)/shard_map/backward_layer/pallas_call | solution.py:732
  225.1 84.4 %weights_back.1 = (bf16[640,4096]{1,0:T(8,128)(2,1)}, bf16[640,4096]{1,0:T(8,128)(2,1)}, bf16[4096,640]{1,0:T(8,128)(2,1)}, bf16[2048,4096]{1,0:T(8,128)(2,1)}, ...) custom-call(bf16[1,2048,640]{2,1,0:T(8,128)(2,1)} %h.5, ...), custom_call_target="tpu_custom_call" | custom-call | tf_op jit(solution)/shard_map/weights_back/pallas_call | solution.py:801
  309.6 70.4 %input_back.1 = (bf16[1,2048,640]{2,1,0:T(8,128)(2,1)}, bf16[80,4096]{1,0:T(8,128)(2,1)}, bf16[80,4096]{1,0:T(8,128)(2,1)}, bf16[512,640]{1,0:T(8,128)(2,1)}) custom-call(bf16[1,2048,640]{2,1,0:T(8,128)(2,1)} %h.5, bf16[2048,640]{1,0:T(8,128)(2,1)} %get-tuple-element.42.dy, bf16[640,4096]{1,0:T(8,128)(2,1)} %bitcast.19, bf16[640,4096]{1,0:T(8,128)(2,1)} %bitcast.21, ...), custom_call_target="tpu_custom_call" | custom-call | tf_op jit(solution)/shard_map/input_back/pallas_call | solution.py:858
  380.0 0.0 copy-start.1
  380.0 0.0 copy-start.2
  380.0 3.5 pad_maximum_fusion
  383.6 0.0 copy-start
  383.6 0.0 copy-done.1
  383.6 0.0 copy-done.2
  383.6 1.2 pad_maximum_fusion.2
  384.8 1.0 copy-done
  385.8 1.5 copy.10
Async XLA Ops:
  380.0 3.5 copy-start.1
  380.0 3.5 copy-start.2
  383.6 2.2 copy-start
